TPU v7x, 256 devices: a 2x2x32 block of a 4x8x32 slice. The times are simulated.
256 devices in a mesh: groups: 4 (over y, x), tile: 64 (over z, core).
Axes of the slice: x: 2, y: 2, z: 32, core: 2. Of those that a mesh axis runs over, the one named last changes fastest.
The devices are a block of a 4x8x32 slice.
Arguments:
- self_query: bfloat16 [32768, 4096], P(('groups', 'tile')), parts along dimension 0, may hold values from -110 to 110
- self_key: bfloat16 [32768, 4096], P(('groups', 'tile')), parts along dimension 0, may hold values from -6 to 6
- self_value: bfloat16 [32768, 4096], P(('groups', 'tile')), parts along dimension 0, may hold values from -24 to 24
- cross_query: bfloat16 [32768, 4096], P(('groups', 'tile')), parts along dimension 0, may hold values from -110 to 110
- text_key: bfloat16 [1024, 4096], P(('groups', 'tile')), parts along dimension 0, may hold values from -6 to 6
- text_value: bfloat16 [1024, 4096], P(('groups', 'tile')), parts along dimension 0, may hold values from -24 to 24
- timestep: int32 [1], replicated, may hold values from 0 to 49
- gate_table: bfloat16 [50, 4096], replicated, may hold values from 0.5 to 2
Outputs:
- mixed: bfloat16 [32768, 4096], P(('groups', 'tile')), parts along dimension 0
There are 4 independent parts, one for each index of `groups`. A program takes and returns all parts, laid end to end along the dimension named above; an argument that names none is the same for every part. Nothing has to cross between parts.
All inputs are finite; a program needn't handle non-finite values.
Results may differ from a plain program's by a relative error of at most 0.0032.
Values may be sent and summed in bfloat16 or wider, within the bound.
No kernel may reach another device: no remote copies, remote signals or barrier semaphores. Data moves between devices by JAX's collectives and lax.ppermute only.
A program may use at most 64 MiB of HBM per device.

v0:
```python
import math

import jax
import jax.numpy as jnp
from jax import lax
from jax.experimental import pallas as pl
from jax.experimental.pallas import tpu as pltpu
from jax.sharding import PartitionSpec as P

HEADS = 32
LOG2E = 1.4426950408889634
SELF_FEATURES = 1024
FEATURES = 1024
KEY_PARTS = 2
VALUE_PARTS = 2
CALLS = 2


def scores_of(queries, keys):
    return lax.dot_general(
        queries, keys, (((1,), (1,)), ((), ())), preferred_element_type=jnp.float32
    )


def self_kernel(bias_ref, step_ref, gate_ref, query_ref, *refs, head_dim):
    key_refs, value_refs, out_ref = refs[:5], refs[5:10], refs[-1]
    scale = LOG2E / math.sqrt(head_dim)
    rows = key_refs[0].shape[0]
    steps = lax.broadcasted_iota(jnp.int32, gate_ref.shape, 0)
    gates = jnp.where(steps == step_ref[0], gate_ref[...].astype(jnp.float32), 0.0)
    gates = jnp.sum(gates, axis=0, keepdims=True)
    for head in range(query_ref.shape[1] // head_dim):
        cols = slice(head * head_dim, (head + 1) * head_dim)
        keys = jnp.concatenate([ref[:, cols] for ref in key_refs], axis=0)
        values = jnp.concatenate([ref[:, cols] for ref in value_refs], axis=0)
        scores = scores_of(query_ref[:, cols], keys)
        scores = jnp.concatenate(
            [scores[:, : 2 * rows]]
            + [scores[:, k * rows : (k + 1) * rows] + bias_ref[k - 2] for k in range(2, 5)],
            axis=1,
        )
        top = jnp.max(scores, axis=1, keepdims=True) * scale
        weights = jnp.exp2(scores * scale - top)
        total = jnp.sum(weights, axis=1, keepdims=True)
        summed = jnp.dot(
            weights.astype(jnp.bfloat16), values, preferred_element_type=jnp.float32
        )
        out_ref[:, cols] = summed * (1.0 / total) * gates[:, cols]


def cross_kernel(core_ref, query_ref, self_ref, *refs, head_dim):
    mine, theirs, out_ref = refs[:8], refs[8:16], refs[16]
    key_buf, value_buf = refs[17], refs[18]
    rows = mine[0].shape[0]
    part = rows // 4

    def fill(keys, values):
        for k in range(8):
            key_buf[k * rows : (k + 1) * rows, :] = keys[k][...]
        for k in range(7):
            value_buf[k * rows : (k + 1) * rows, :] = values[k][...]
        for to, source in enumerate((1, 3, 0, 2)):
            first = 7 * rows + to * part
            value_buf[first : first + part, :] = values[7][source * part : (source + 1) * part, :]

    @pl.when(core_ref[0] == 0)
    def _():
        fill(mine, theirs)

    @pl.when(core_ref[0] != 0)
    def _():
        fill(theirs, mine)

    scale = LOG2E / math.sqrt(head_dim)
    for head in range(query_ref.shape[1] // head_dim):
        cols = slice(head * head_dim, (head + 1) * head_dim)
        scores = scores_of(query_ref[:, cols], key_buf[:, cols])
        top = jnp.max(scores, axis=1, keepdims=True) * scale
        weights = jnp.exp2(scores * scale - top)
        total = jnp.sum(weights, axis=1, keepdims=True)
        summed = jnp.dot(
            weights.astype(jnp.bfloat16), value_buf[:, cols], preferred_element_type=jnp.float32
        )
        out_ref[:, cols] = (self_ref[:, cols] + summed * (1.0 / total)).astype(out_ref.dtype)


def self_attention(bias, timestep, gates, queries, keys, values, first, width, partial):
    rows, whole = queries.shape
    features = min(SELF_FEATURES, width)
    offset = first // features

    def block_of(array):
        skip = first % array.shape[1] // features
        return pl.BlockSpec((array.shape[0], features), lambda i: (0, i + skip))

    arrays = (gates, queries, *keys, *values)
    in_specs = [pl.BlockSpec(memory_space=pltpu.SMEM)] * 2 + [block_of(array) for array in arrays]
    aliases = {}
    if partial is not None:
        aliases = {len(in_specs): 0}
        in_specs.append(pl.BlockSpec(memory_space=pl.ANY))
        arrays += (partial,)
    return pl.pallas_call(
        lambda *refs: self_kernel(*refs, head_dim=whole // HEADS),
        grid=(width // features,),
        in_specs=in_specs,
        out_specs=pl.BlockSpec((rows, features), lambda i: (0, i + offset)),
        out_shape=jax.ShapeDtypeStruct((rows, whole), jnp.float32),
        input_output_aliases=aliases,
        name="self_attention",
    )(bias, timestep, *arrays)


def cross_attention(core, queries, self_part, mine, theirs):
    rows, width = queries.shape
    text_rows = sum(piece.shape[0] for piece in mine)
    block = pl.BlockSpec((rows, FEATURES), lambda i: (0, i))
    piece_block = pl.BlockSpec((mine[0].shape[0], FEATURES), lambda i: (0, i))
    return pl.pallas_call(
        lambda *refs: cross_kernel(*refs, head_dim=width // HEADS),
        grid=(width // FEATURES,),
        in_specs=[pl.BlockSpec(memory_space=pltpu.SMEM), block, block] + [piece_block] * 16,
        out_specs=block,
        out_shape=jax.ShapeDtypeStruct((rows, width), queries.dtype),
        scratch_shapes=[pltpu.VMEM((text_rows, FEATURES), queries.dtype)] * 2,
        name="cross_attention",
    )(core, queries, self_part, *mine, *theirs)


def shards(
    self_query, self_key, self_value, cross_query, text_key, text_value, timestep, gate_table
):
    tiles = lax.axis_size("tile")
    chips = tiles // 2
    stride = chips // 4
    place = lax.axis_index("tile")
    core = place % 2
    width = self_query.shape[1]
    first = core == 0

    def send(block, route):
        return lax.ppermute(block, "tile", route)

    def from_chip(block, distance):
        return send(block, [(i, (i + 2 * distance) % tiles) for i in range(tiles)])

    def in_window(block, shift):
        return send(block, [(i, i + shift) for i in range(tiles) if 0 <= i + shift < tiles])

    def partner(block):
        return send(block, [(i, i ^ 1) for i in range(tiles)])

    def by_core(block, distance):
        route = [(i, (i + 2 * distance) % tiles) for i in range(0, tiles, 2)]
        route += [(i, (i - 2 * distance) % tiles) for i in range(1, tiles, 2)]
        return send(block, route)

    key_partner, value_partner = partner(self_key), partner(self_value)

    their_key, their_value = partner(text_key), partner(text_value)
    block = jnp.where(
        first,
        jnp.concatenate([text_key, their_key], axis=0),
        jnp.concatenate([their_value, text_value], axis=0),
    )
    block_below, block_above = from_chip(block, stride), from_chip(block, -stride)
    block_far = by_core(jnp.where(first, block_below, block_above), stride)
    gathered = jnp.concatenate([block, block_below, block_above, block_far], axis=0)
    lower, upper = [gathered], [gathered]
    for _ in range(1, stride // 2):
        lower.append(from_chip(lower[-1], 1))
        upper.append(from_chip(upper[-1], -1))
    last = by_core(jnp.where(first, lower[-1], upper[-1]), 1)
    pieces = [gathered, *lower[1:], *upper[1:], last]
    their_pieces = [partner(piece) for piece in pieces]

    step = jnp.where(first, -1, 1)
    position = jnp.stack([place - 2, place + 2, place + step])
    bias = jnp.where((position >= 0) & (position < tiles), 0.0, -1e30).astype(jnp.float32)

    def window_of(array, parts):
        span = width // parts
        pieces = []
        for part in range(parts):
            if part > 0:
                array, _ = lax.optimization_barrier((array, block_below))
            piece = lax.slice_in_dim(array, part * span, (part + 1) * span, axis=1)
            below = in_window(piece, 2)
            above = in_window(piece, -2)
            following = partner(jnp.where(first, above, below))
            pieces.append((below, above, following))
        return pieces

    keys = window_of(self_key, KEY_PARTS)
    values = window_of(self_value, VALUE_PARTS)
    self_part = None
    share = width // CALLS
    for call in range(CALLS):
        self_part = self_attention(
            bias,
            timestep,
            gate_table,
            self_query,
            (self_key, key_partner, *keys[call * KEY_PARTS // CALLS]),
            (self_value, value_partner, *values[call * VALUE_PARTS // CALLS]),
            call * share,
            share,
            self_part,
        )
    return cross_attention(core[None], cross_query, self_part, pieces, their_pieces)


def solution(mesh):
    rows = P(("groups", "tile"), None)
    return jax.shard_map(
        shards,
        mesh=mesh,
        in_specs=(rows,) * 6 + (P(), P()),
        out_specs=rows,
        check_vma=False,
    )
```

profile of v0, /device:TPU:37, one launch (start us, length us, event | category | flops | bytes accessed | tf_op | source)
XLA Modules:
  0.0 164.1 jit_solution(7246499375768597292)
XLA Ops:
  0.0 20.4 %collective-permute-start.1 = (bf16[4,4096]{1,0:T(4,128)(2,1)}, bf16[4,4096]{1,0:T(4,128)(2,1)S(1)}, u32[]{:S(2)}, u32[]{:S(2)}) collective-permute-start(bf16[4,4096]{1,0:T(4,128)(2,1)} %param.12), channel_id=1, source_target_pairs={{0,1},{1,0},{2,3},{3,2},{4,5},{5,4},{6,7},{7,6},{8,9},{9,8},{10,11... | collective-permute-start | bytes 98312 | tf_op jit(solution)/shard_map/ppermute | solution.py:142
  20.4 1.1 collective-permute-done.1
  21.5 0.3 collective-permute-done.2
  21.8 0.8 maximum_select_fusion
  22.8 10.2 %collective-permute-start.17 = (bf16[8,4096]{1,0:T(8,128)(2,1)S(1)}, bf16[8,4096]{1,0:T(8,128)(2,1)S(1)}, u32[]{:S(2)}, u32[]{:S(2)}) collective-permute-start(bf16[8,4096]{1,0:T(8,128)(2,1)S(1)} %maximum_select_fusion), channel_id=1, source_target_pairs={{0,48},{1,49},{2,50},{3,51},{4,52},{5,53},{6,54},{7,55},{8,56},{9,... | collective-permute-start | bytes 196616 | tf_op jit(solution)/shard_map/ppermute | solution.py:142
  33.0 2.0 %collective-permute-done.3 = bf16[8,4096]{1,0:T(8,128)(2,1)S(1)} collective-permute-done((bf16[8,4096]{1,0:T(8,128)(2,1)S(1)}, bf16[8,4096]{1,0:T(8,128)(2,1)S(1)}, u32[]{:S(2)}, u32[]{:S(2)}) %collective-permute-start.3) | collective-permute-done | bytes 65568 | tf_op jit(solution)/shard_map/ppermute | solution.py:142
  35.0 10.4 %collective-permute-done.17 = bf16[8,4096]{1,0:T(8,128)(2,1)S(1)} collective-permute-done((bf16[8,4096]{1,0:T(8,128)(2,1)S(1)}, bf16[8,4096]{1,0:T(8,128)(2,1)S(1)}, u32[]{:S(2)}, u32[]{:S(2)}) %collective-permute-start.17) | collective-permute-done | bytes 65568 | tf_op jit(solution)/shard_map/ppermute | solution.py:142
  45.4 4.6 %collective-permute-start.18 = (bf16[8,4096]{1,0:T(8,128)(2,1)S(1)}, bf16[8,4096]{1,0:T(8,128)(2,1)S(1)}, u32[]{:S(2)}, u32[]{:S(2)}) collective-permute-start(bf16[8,4096]{1,0:T(8,128)(2,1)S(1)} %broadcast_select_fusion.5), channel_id=1, source_target_pairs={{0,16},{2,18},{4,20},{6,22},{8,24},{10,26},{12,28},{14,30},{16,32}... | collective-permute-start | bytes 196616 | tf_op jit(solution)/shard_map/ppermute | solution.py:142
  50.0 1.1 slice.14
  51.1 3.6 %collective-permute-start.11 = (bf16[128,2048]{1,0:T(8,128)(2,1)S(1)}, bf16[128,2048]{1,0:T(8,128)(2,1)S(1)}, u32[]{:S(2)}, u32[]{:S(2)}) collective-permute-start(bf16[128,2048]{1,0:T(8,128)(2,1)S(1)} %slice.14), channel_id=1, source_target_pairs={{0,2},{1,3},{2,4},{3,5},{4,6},{5,7},{6,8},{7,9},{8,10},{9,11},{10,... | collective-permute-start | bytes 1572872 | tf_op jit(solution)/shard_map/ppermute | solution.py:142
  54.7 1.3 collective-permute-start.12
  56.0 1.8 %collective-permute-done.18 = bf16[8,4096]{1,0:T(8,128)(2,1)S(1)} collective-permute-done((bf16[8,4096]{1,0:T(8,128)(2,1)S(1)}, bf16[8,4096]{1,0:T(8,128)(2,1)S(1)}, u32[]{:S(2)}, u32[]{:S(2)}) %collective-permute-start.18) | collective-permute-done | bytes 65568 | tf_op jit(solution)/shard_map/ppermute | solution.py:142
  57.8 1.1 collective-permute-start.19
  59.0 1.1 slice.15
  60.0 3.3 %collective-permute-start.14 = (bf16[128,2048]{1,0:T(8,128)(2,1)S(1)}, bf16[128,2048]{1,0:T(8,128)(2,1)S(1)}, u32[]{:S(2)}, u32[]{:S(2)}) collective-permute-start(bf16[128,2048]{1,0:T(8,128)(2,1)S(1)} %slice.15), channel_id=1, source_target_pairs={{0,2},{1,3},{2,4},{3,5},{4,6},{5,7},{6,8},{7,9},{8,10},{9,11},{10,... | collective-permute-start | bytes 1572872 | tf_op jit(solution)/shard_map/ppermute | solution.py:142
  63.3 1.3 collective-permute-start.15
  64.7 6.4 %collective-permute-done.19.refs_4_ = bf16[32,4096]{1,0:T(8,128)(2,1)S(1)} collective-permute-done((bf16[32,4096]{1,0:T(8,128)(2,1)S(1)}, bf16[32,4096]{1,0:T(8,128)(2,1)S(1)}, u32[]{:S(2)}, u32[]{:S(2)}) %collective-permute-start.19) | collective-permute-done | bytes 262176 | tf_op jit(solution)/shard_map/ppermute | solution.py:142
  71.2 4.2 %collective-permute-start.8 = (bf16[128,2048]{1,0:T(8,128)(2,1)S(1)}, bf16[128,2048]{1,0:T(8,128)(2,1)S(1)}, u32[]{:S(2)}, u32[]{:S(2)}) collective-permute-start(bf16[128,2048]{1,0:T(8,128)(2,1)S(1)} %slice.13), channel_id=1, source_target_pairs={{0,2},{1,3},{2,4},{3,5},{4,6},{5,7},{6,8},{7,9},{8,10},{9,11},{10,... | collective-permute-start | bytes 1572872 | tf_op jit(solution)/shard_map/ppermute | solution.py:142
  75.4 1.3 collective-permute-start.9
  76.7 7.9 %collective-permute-start.22 = (bf16[32,4096]{1,0:T(8,128)(2,1)S(1)}, bf16[32,4096]{1,0:T(8,128)(2,1)S(1)}, u32[]{:S(2)}, u32[]{:S(2)}) collective-permute-start(bf16[32,4096]{1,0:T(8,128)(2,1)S(1)} %pad_maximum_fusion.refs_3_), channel_id=1, source_target_pairs={{0,62},{1,63},{2,0},{3,1},{4,2},{5,3},{6,4},{7,5},{8,6},{9,7},{10,... | collective-permute-start | bytes 786440 | tf_op jit(solution)/shard_map/ppermute | solution.py:142
  84.7 11.2 %collective-permute-done.22.refs_7_ = bf16[32,4096]{1,0:T(8,128)(2,1)S(1)} collective-permute-done((bf16[32,4096]{1,0:T(8,128)(2,1)S(1)}, bf16[32,4096]{1,0:T(8,128)(2,1)S(1)}, u32[]{:S(2)}, u32[]{:S(2)}) %collective-permute-start.22) | collective-permute-done | bytes 262176 | tf_op jit(solution)/shard_map/ppermute | solution.py:142
  95.9 4.1 %collective-permute-start.4 = (bf16[128,2048]{1,0:T(8,128)(2,1)S(1)}, bf16[128,2048]{1,0:T(8,128)(2,1)S(1)}, u32[]{:S(2)}, u32[]{:S(2)}) collective-permute-start(bf16[128,2048]{1,0:T(8,128)(2,1)S(1)} %slice.12), channel_id=1, source_target_pairs={{0,2},{1,3},{2,4},{3,5},{4,6},{5,7},{6,8},{7,9},{8,10},{9,11},{10,... | collective-permute-start | bytes 1572872 | tf_op jit(solution)/shard_map/ppermute | solution.py:142
  100.0 1.3 collective-permute-start.5
  101.3 3.4 %collective-permute-start.26 = (bf16[32,4096]{1,0:T(8,128)(2,1)S(1)}, bf16[32,4096]{1,0:T(8,128)(2,1)S(1)}, u32[]{:S(2)}, u32[]{:S(2)}) collective-permute-start(bf16[32,4096]{1,0:T(8,128)(2,1)S(1)} %pad_maximum_fusion.refs_3_), channel_id=1, source_target_pairs={{0,1},{1,0},{2,3},{3,2},{4,5},{5,4},{6,7},{7,6},{8,9},{9,8},{10,11... | collective-permute-start | bytes 786440 | tf_op jit(solution)/shard_map/ppermute | solution.py:142
  104.8 1.1 collective-permute-done.26.refs_11_
  105.9 2.4 %collective-permute-start.20 = (bf16[32,4096]{1,0:T(8,128)(2,1)S(1)}, bf16[32,4096]{1,0:T(8,128)(2,1)}, u32[]{:S(2)}, u32[]{:S(2)}) collective-permute-start(bf16[32,4096]{1,0:T(8,128)(2,1)S(1)} %collective-permute-done.19.refs_4_), channel_id=1, source_target_pairs={{0,2},{1,3},{2,4},{3,5},{4,6},{5,7},{6,8},{7,9},{8,10},{9,11},{10,... | collective-permute-start | bytes 786440 | tf_op jit(solution)/shard_map/ppermute | solution.py:142
  108.3 0.3 collective-permute-start.23
  108.6 0.9 collective-permute-start.13
  109.7 5.2 %collective-permute-start.27 = (bf16[32,4096]{1,0:T(8,128)(2,1)S(1)}, bf16[32,4096]{1,0:T(8,128)(2,1)}, u32[]{:S(2)}, u32[]{:S(2)}) collective-permute-start(bf16[32,4096]{1,0:T(8,128)(2,1)S(1)} %collective-permute-done.19.refs_4_), channel_id=1, source_target_pairs={{0,1},{1,0},{2,3},{3,2},{4,5},{5,4},{6,7},{7,6},{8,9},{9,8},{10,11... | collective-permute-start | bytes 786440 | tf_op jit(solution)/shard_map/ppermute | solution.py:142
  114.9 4.2 %collective-permute-start.30 = (bf16[32,4096]{1,0:T(8,128)(2,1)S(1)}, bf16[32,4096]{1,0:T(8,128)(2,1)S(1)}, u32[]{:S(2)}, u32[]{:S(2)}) collective-permute-start(bf16[32,4096]{1,0:T(8,128)(2,1)S(1)} %collective-permute-done.22.refs_7_), channel_id=1, source_target_pairs={{0,1},{1,0},{2,3},{3,2},{4,5},{5,4},{6,7},{7,6},{8,9},{9,8},{10,11... | collective-permute-start | bytes 786440 | tf_op jit(solution)/shard_map/ppermute | solution.py:142
  119.1 2.7 %collective-permute-start.24 = (bf16[32,4096]{1,0:T(8,128)(2,1)}, bf16[32,4096]{1,0:T(8,128)(2,1)}, u32[]{:S(2)}, u32[]{:S(2)}) collective-permute-start(bf16[32,4096]{1,0:T(8,128)(2,1)} %collective-permute-done.23.refs_8_), channel_id=1, source_target_pairs={{0,62},{1,63},{2,0},{3,1},{4,2},{5,3},{6,4},{7,5},{8,6},{9,7},{10,... | collective-permute-start | bytes 786440 | tf_op jit(solution)/shard_map/ppermute | solution.py:142
  121.9 0.8 collective-permute-start
  122.8 0.5 copy-done.21
  123.4 4.9 %collective-permute-done.21.refs_6_ = bf16[32,4096]{1,0:T(8,128)(2,1)S(1)} collective-permute-done((bf16[32,4096]{1,0:T(8,128)(2,1)}, bf16[32,4096]{1,0:T(8,128)(2,1)S(1)}, u32[]{:S(2)}, u32[]{:S(2)}) %collective-permute-start.21) | collective-permute-done | bytes 262176 | tf_op jit(solution)/shard_map/ppermute | solution.py:142
  128.2 1.0 collective-permute-start.16
  129.4 0.4 collective-permute-start.6
  129.7 1.0 broadcast_select_fusion.4
  130.8 2.6 %collective-permute-start.25 = (bf16[32,4096]{1,0:T(8,128)(2,1)S(1)}, bf16[32,4096]{1,0:T(8,128)(2,1)}, u32[]{:S(2)}, u32[]{:S(2)}) collective-permute-start(bf16[32,4096]{1,0:T(8,128)(2,1)S(1)} %broadcast_select_fusion.4), channel_id=1, source_target_pairs={{0,2},{2,4},{4,6},{6,8},{8,10},{10,12},{12,14},{14,16},{16,18},{18... | collective-permute-start | bytes 786440 | tf_op jit(solution)/shard_map/ppermute | solution.py:142
  133.4 1.0 copy-done.3
  134.4 0.5 collective-permute-start.31
  135.0 0.6 collective-permute-start.32
  135.6 1.0 collective-permute-done.25.refs_10_
  136.7 2.3 %collective-permute-start.33 = (bf16[32,4096]{1,0:T(8,128)(2,1)}, bf16[32,4096]{1,0:T(8,128)(2,1)S(1)}, u32[]{:S(2)}, u32[]{:S(2)}) collective-permute-start(bf16[32,4096]{1,0:T(8,128)(2,1)} %collective-permute-done.25.refs_10_), channel_id=1, source_target_pairs={{0,1},{1,0},{2,3},{3,2},{4,5},{5,4},{6,7},{7,6},{8,9},{9,8},{10,11... | collective-permute-start | bytes 786440 | tf_op jit(solution)/shard_map/ppermute | solution.py:142
  139.6 0.7 and_select_fusion.refs_0_
  140.3 8.0 %self_attention.2.refs_14_ = f32[128,4096]{1,0:T(8,128)} custom-call(f32[3]{0:T(128)} %and_select_fusion.refs_0_, s32[1]{0:T(128)S(6)} %copy.11.refs_1_, bf16[50,4096]{1,0:T(8,128)(2,1)} %refs_2_.3, bf16[128,4096]{1,0:T(8,128)(2,1)} %refs_3_.3, bf16[128,4096]{1,0:T(8,128)(2,1)} %refs_4_.3, bf16[128,4096]{1,0:T(8,128)(2,1)} %copy-done.2, ...), custom_call_target="tpu_custom_call" | custom-call | tf_op jit(solution)/shard_map/self_attention/pallas_call | solution.py:103
  148.3 8.0 %self_attention.3.refs_2_ = f32[128,4096]{1,0:T(8,128)} custom-call(f32[3]{0:T(128)} %and_select_fusion.refs_0_, s32[1]{0:T(128)S(6)} %copy.11.refs_1_, bf16[50,4096]{1,0:T(8,128)(2,1)} %refs_2_.3, bf16[128,4096]{1,0:T(8,128)(2,1)} %refs_3_.3, bf16[128,4096]{1,0:T(8,128)(2,1)} %refs_4_.3, ...), custom_call_target="tpu_custom_call", output_to_operand_aliasing={{}: (14, {})} | custom-call | tf_op jit(solution)/shard_map/self_attention/pallas_call | solution.py:103
  156.4 0.6 copy-done.22
  157.4 6.5 %cross_attention.1 = bf16[128,4096]{1,0:T(8,128)(2,1)} custom-call(s32[1]{0:T(128)} %bitcast.refs_0_, bf16[128,4096]{1,0:T(8,128)(2,1)} %refs_1_.3, f32[128,4096]{1,0:T(8,128)} %self_attention.3.refs_2_, bf16[32,4096]{1,0:T(8,128)(2,1)} %copy-done.12, bf16[32,4096]{1,0:T(8,128)(2,1)} %copy-done.18, bf16[32,4096]{1,0:T(8,128)(2,1)} %collective-permute-done.20.refs_5_, ...), custom_call_target="tpu_custom_call" | custom-call | tf_op jit(solution)/shard_map/cross_attention/pallas_call | solution.py:119
  (90 shorter events, 1.5 us)
Async XLA Ops:
  0.0 64.7 %copy-start = (bf16[128,4096]{1,0:T(8,128)(2,1)S(1)}, bf16[128,4096]{1,0:T(8,128)(2,1)}, u32[]{:S(2)}) copy-start(bf16[128,4096]{1,0:T(8,128)(2,1)} %refs_4_.3) | copy-start | bytes 3145732
  0.0 64.6 %copy-start.1 = (bf16[128,4096]{1,0:T(8,128)(2,1)S(1)}, bf16[128,4096]{1,0:T(8,128)(2,1)}, u32[]{:S(2)}) copy-start(bf16[128,4096]{1,0:T(8,128)(2,1)} %refs_9_.3) | copy-start | bytes 3145732
  0.0 21.5 %collective-permute-start.1 = (bf16[4,4096]{1,0:T(4,128)(2,1)}, bf16[4,4096]{1,0:T(4,128)(2,1)S(1)}, u32[]{:S(2)}, u32[]{:S(2)}) collective-permute-start(bf16[4,4096]{1,0:T(4,128)(2,1)} %param.12), channel_id=1, source_target_pairs={{0,1},{1,0},{2,3},{3,2},{4,5},{5,4},{6,7},{7,6},{8,9},{9,8},{10,11... | collective-permute-start | bytes 98312 | tf_op jit(solution)/shard_map/ppermute | solution.py:142
  20.4 1.4 collective-permute-start.2
  22.7 12.3 %collective-permute-start.3 = (bf16[8,4096]{1,0:T(8,128)(2,1)S(1)}, bf16[8,4096]{1,0:T(8,128)(2,1)S(1)}, u32[]{:S(2)}, u32[]{:S(2)}) collective-permute-start(bf16[8,4096]{1,0:T(8,128)(2,1)S(1)} %maximum_select_fusion), channel_id=1, source_target_pairs={{0,16},{1,17},{2,18},{3,19},{4,20},{5,21},{6,22},{7,23},{8,24},{9,... | collective-permute-start | bytes 196616 | tf_op jit(solution)/shard_map/ppermute | solution.py:142
  22.8 22.6 %collective-permute-start.17 = (bf16[8,4096]{1,0:T(8,128)(2,1)S(1)}, bf16[8,4096]{1,0:T(8,128)(2,1)S(1)}, u32[]{:S(2)}, u32[]{:S(2)}) collective-permute-start(bf16[8,4096]{1,0:T(8,128)(2,1)S(1)} %maximum_select_fusion), channel_id=1, source_target_pairs={{0,48},{1,49},{2,50},{3,51},{4,52},{5,53},{6,54},{7,55},{8,56},{9,... | collective-permute-start | bytes 196616 | tf_op jit(solution)/shard_map/ppermute | solution.py:142
  45.4 12.4 %collective-permute-start.18 = (bf16[8,4096]{1,0:T(8,128)(2,1)S(1)}, bf16[8,4096]{1,0:T(8,128)(2,1)S(1)}, u32[]{:S(2)}, u32[]{:S(2)}) collective-permute-start(bf16[8,4096]{1,0:T(8,128)(2,1)S(1)} %broadcast_select_fusion.5), channel_id=1, source_target_pairs={{0,16},{2,18},{4,20},{6,22},{8,24},{10,26},{12,28},{14,30},{16,32}... | collective-permute-start | bytes 196616 | tf_op jit(solution)/shard_map/ppermute | solution.py:142
  51.1 24.3 %collective-permute-start.11 = (bf16[128,2048]{1,0:T(8,128)(2,1)S(1)}, bf16[128,2048]{1,0:T(8,128)(2,1)S(1)}, u32[]{:S(2)}, u32[]{:S(2)}) collective-permute-start(bf16[128,2048]{1,0:T(8,128)(2,1)S(1)} %slice.14), channel_id=1, source_target_pairs={{0,2},{1,3},{2,4},{3,5},{4,6},{5,7},{6,8},{7,9},{8,10},{9,11},{10,... | collective-permute-start | bytes 1572872 | tf_op jit(solution)/shard_map/ppermute | solution.py:142
  54.7 21.9 %collective-permute-start.12 = (bf16[128,2048]{1,0:T(8,128)(2,1)S(1)}, bf16[128,2048]{1,0:T(8,128)(2,1)S(1)}, u32[]{:S(2)}, u32[]{:S(2)}) collective-permute-start(bf16[128,2048]{1,0:T(8,128)(2,1)S(1)} %slice.14), channel_id=1, source_target_pairs={{2,0},{3,1},{4,2},{5,3},{6,4},{7,5},{8,6},{9,7},{10,8},{11,9},{12,... | collective-permute-start | bytes 1572872 | tf_op jit(solution)/shard_map/ppermute | solution.py:142
  57.8 43.5 %copy-start.12 = (bf16[32,4096]{1,0:T(8,128)(2,1)}, bf16[32,4096]{1,0:T(8,128)(2,1)S(1)}, u32[]{:S(2)}) copy-start(bf16[32,4096]{1,0:T(8,128)(2,1)S(1)} %pad_maximum_fusion.refs_3_) | copy-start | bytes 786436
  57.8 13.3 %collective-permute-start.19 = (bf16[32,4096]{1,0:T(8,128)(2,1)S(1)}, bf16[32,4096]{1,0:T(8,128)(2,1)S(1)}, u32[]{:S(2)}, u32[]{:S(2)}) collective-permute-start(bf16[32,4096]{1,0:T(8,128)(2,1)S(1)} %pad_maximum_fusion.refs_3_), channel_id=1, source_target_pairs={{0,2},{1,3},{2,4},{3,5},{4,6},{5,7},{6,8},{7,9},{8,10},{9,11},{10,... | collective-permute-start | bytes 786440 | tf_op jit(solution)/shard_map/ppermute | solution.py:142
  60.0 40.0 %collective-permute-start.14 = (bf16[128,2048]{1,0:T(8,128)(2,1)S(1)}, bf16[128,2048]{1,0:T(8,128)(2,1)S(1)}, u32[]{:S(2)}, u32[]{:S(2)}) collective-permute-start(bf16[128,2048]{1,0:T(8,128)(2,1)S(1)} %slice.15), channel_id=1, source_target_pairs={{0,2},{1,3},{2,4},{3,5},{4,6},{5,7},{6,8},{7,9},{8,10},{9,11},{10,... | collective-permute-start | bytes 1572872 | tf_op jit(solution)/shard_map/ppermute | solution.py:142
  63.3 38.0 %collective-permute-start.15 = (bf16[128,2048]{1,0:T(8,128)(2,1)S(1)}, bf16[128,2048]{1,0:T(8,128)(2,1)S(1)}, u32[]{:S(2)}, u32[]{:S(2)}) collective-permute-start(bf16[128,2048]{1,0:T(8,128)(2,1)S(1)} %slice.15), channel_id=1, source_target_pairs={{2,0},{3,1},{4,2},{5,3},{6,4},{7,5},{8,6},{9,7},{10,8},{11,9},{12,... | collective-permute-start | bytes 1572872 | tf_op jit(solution)/shard_map/ppermute | solution.py:142
  71.2 38.5 %copy-start.18 = (bf16[32,4096]{1,0:T(8,128)(2,1)}, bf16[32,4096]{1,0:T(8,128)(2,1)S(1)}, u32[]{:S(2)}) copy-start(bf16[32,4096]{1,0:T(8,128)(2,1)S(1)} %collective-permute-done.19.refs_4_) | copy-start | bytes 786436
  71.2 37.2 %collective-permute-start.8 = (bf16[128,2048]{1,0:T(8,128)(2,1)S(1)}, bf16[128,2048]{1,0:T(8,128)(2,1)S(1)}, u32[]{:S(2)}, u32[]{:S(2)}) collective-permute-start(bf16[128,2048]{1,0:T(8,128)(2,1)S(1)} %slice.13), channel_id=1, source_target_pairs={{0,2},{1,3},{2,4},{3,5},{4,6},{5,7},{6,8},{7,9},{8,10},{9,11},{10,... | collective-permute-start | bytes 1572872 | tf_op jit(solution)/shard_map/ppermute | solution.py:142
  75.3 34.3 %copy-start.4 = (bf16[128,2048]{1,0:T(8,128)(2,1)}, bf16[128,2048]{1,0:T(8,128)(2,1)S(1)}, u32[]{:S(2)}) copy-start(bf16[128,2048]{1,0:T(8,128)(2,1)S(1)} %collective-permute-done.11.refs_6_) | copy-start | bytes 1572868
  75.4 33.3 %collective-permute-start.9 = (bf16[128,2048]{1,0:T(8,128)(2,1)S(1)}, bf16[128,2048]{1,0:T(8,128)(2,1)S(1)}, u32[]{:S(2)}, u32[]{:S(2)}) collective-permute-start(bf16[128,2048]{1,0:T(8,128)(2,1)S(1)} %slice.13), channel_id=1, source_target_pairs={{2,0},{3,1},{4,2},{5,3},{6,4},{7,5},{8,6},{9,7},{10,8},{11,9},{12,... | collective-permute-start | bytes 1572872 | tf_op jit(solution)/shard_map/ppermute | solution.py:142
  76.7 33.0 %copy-start.5 = (bf16[128,2048]{1,0:T(8,128)(2,1)}, bf16[128,2048]{1,0:T(8,128)(2,1)S(1)}, u32[]{:S(2)}) copy-start(bf16[128,2048]{1,0:T(8,128)(2,1)S(1)} %collective-permute-done.12.refs_7_) | copy-start | bytes 1572868
  76.7 19.2 %collective-permute-start.22 = (bf16[32,4096]{1,0:T(8,128)(2,1)S(1)}, bf16[32,4096]{1,0:T(8,128)(2,1)S(1)}, u32[]{:S(2)}, u32[]{:S(2)}) collective-permute-start(bf16[32,4096]{1,0:T(8,128)(2,1)S(1)} %pad_maximum_fusion.refs_3_), channel_id=1, source_target_pairs={{0,62},{1,63},{2,0},{3,1},{4,2},{5,3},{6,4},{7,5},{8,6},{9,7},{10,... | collective-permute-start | bytes 786440 | tf_op jit(solution)/shard_map/ppermute | solution.py:142
  95.9 25.9 %copy-start.19 = (bf16[32,4096]{1,0:T(8,128)(2,1)}, bf16[32,4096]{1,0:T(8,128)(2,1)S(1)}, u32[]{:S(2)}) copy-start(bf16[32,4096]{1,0:T(8,128)(2,1)S(1)} %collective-permute-done.22.refs_7_) | copy-start | bytes 786436
  95.9 13.8 %collective-permute-start.4 = (bf16[128,2048]{1,0:T(8,128)(2,1)S(1)}, bf16[128,2048]{1,0:T(8,128)(2,1)S(1)}, u32[]{:S(2)}, u32[]{:S(2)}) collective-permute-start(bf16[128,2048]{1,0:T(8,128)(2,1)S(1)} %slice.12), channel_id=1, source_target_pairs={{0,2},{1,3},{2,4},{3,5},{4,6},{5,7},{6,8},{7,9},{8,10},{9,11},{10,... | collective-permute-start | bytes 1572872 | tf_op jit(solution)/shard_map/ppermute | solution.py:142
  100.0 21.8 %copy-start.6 = (bf16[128,2048]{1,0:T(8,128)(2,1)}, bf16[128,2048]{1,0:T(8,128)(2,1)S(1)}, u32[]{:S(2)}) copy-start(bf16[128,2048]{1,0:T(8,128)(2,1)S(1)} %collective-permute-done.14.refs_11_) | copy-start | bytes 1572868
  100.0 14.9 %collective-permute-start.5 = (bf16[128,2048]{1,0:T(8,128)(2,1)S(1)}, bf16[128,2048]{1,0:T(8,128)(2,1)S(1)}, u32[]{:S(2)}, u32[]{:S(2)}) collective-permute-start(bf16[128,2048]{1,0:T(8,128)(2,1)S(1)} %slice.12), channel_id=1, source_target_pairs={{2,0},{3,1},{4,2},{5,3},{6,4},{7,5},{8,6},{9,7},{10,8},{11,9},{12,... | collective-permute-start | bytes 1572872 | tf_op jit(solution)/shard_map/ppermute | solution.py:142
  101.3 20.5 %copy-start.7 = (bf16[128,2048]{1,0:T(8,128)(2,1)}, bf16[128,2048]{1,0:T(8,128)(2,1)S(1)}, u32[]{:S(2)}) copy-start(bf16[128,2048]{1,0:T(8,128)(2,1)S(1)} %collective-permute-done.15.refs_12_) | copy-start | bytes 1572868
  101.3 4.6 %collective-permute-start.26 = (bf16[32,4096]{1,0:T(8,128)(2,1)S(1)}, bf16[32,4096]{1,0:T(8,128)(2,1)S(1)}, u32[]{:S(2)}, u32[]{:S(2)}) collective-permute-start(bf16[32,4096]{1,0:T(8,128)(2,1)S(1)} %pad_maximum_fusion.refs_3_), channel_id=1, source_target_pairs={{0,1},{1,0},{2,3},{3,2},{4,5},{5,4},{6,7},{7,6},{8,9},{9,8},{10,11... | collective-permute-start | bytes 786440 | tf_op jit(solution)/shard_map/ppermute | solution.py:142
  105.9 13.1 %collective-permute-start.20 = (bf16[32,4096]{1,0:T(8,128)(2,1)S(1)}, bf16[32,4096]{1,0:T(8,128)(2,1)}, u32[]{:S(2)}, u32[]{:S(2)}) collective-permute-start(bf16[32,4096]{1,0:T(8,128)(2,1)S(1)} %collective-permute-done.19.refs_4_), channel_id=1, source_target_pairs={{0,2},{1,3},{2,4},{3,5},{4,6},{5,7},{6,8},{7,9},{8,10},{9,11},{10,... | collective-permute-start | bytes 786440 | tf_op jit(solution)/shard_map/ppermute | solution.py:142
  108.3 26.5 %copy-start.8 = (bf16[128,2048]{1,0:T(8,128)(2,1)}, bf16[128,2048]{1,0:T(8,128)(2,1)S(1)}, u32[]{:S(2)}) copy-start(bf16[128,2048]{1,0:T(8,128)(2,1)S(1)} %collective-permute-done.8.refs_11_) | copy-start | bytes 1572868
  108.3 10.8 %collective-permute-start.23 = (bf16[32,4096]{1,0:T(8,128)(2,1)S(1)}, bf16[32,4096]{1,0:T(8,128)(2,1)}, u32[]{:S(2)}, u32[]{:S(2)}) collective-permute-start(bf16[32,4096]{1,0:T(8,128)(2,1)S(1)} %collective-permute-done.22.refs_7_), channel_id=1, source_target_pairs={{0,62},{1,63},{2,0},{3,1},{4,2},{5,3},{6,4},{7,5},{8,6},{9,7},{10,... | collective-permute-start | bytes 786440 | tf_op jit(solution)/shard_map/ppermute | solution.py:142
  108.6 26.2 %copy-start.9 = (bf16[128,2048]{1,0:T(8,128)(2,1)}, bf16[128,2048]{1,0:T(8,128)(2,1)S(1)}, u32[]{:S(2)}) copy-start(bf16[128,2048]{1,0:T(8,128)(2,1)S(1)} %collective-permute-done.9.refs_12_) | copy-start | bytes 1572868
  108.6 20.7 %collective-permute-start.13 = (bf16[128,2048]{1,0:T(8,128)(2,1)S(1)}, bf16[128,2048]{1,0:T(8,128)(2,1)S(1)}, u32[]{:S(2)}, u32[]{:S(2)}) collective-permute-start(bf16[128,2048]{1,0:T(8,128)(2,1)S(1)} %broadcast_select_fusion.1), channel_id=1, source_target_pairs={{0,1},{1,0},{2,3},{3,2},{4,5},{5,4},{6,7},{7,6},{8,9},{9,8},{10,11... | collective-permute-start | bytes 1572872 | tf_op jit(solution)/shard_map/ppermute | solution.py:142
  109.7 25.4 %copy-start.10 = (bf16[128,2048]{1,0:T(8,128)(2,1)}, bf16[128,2048]{1,0:T(8,128)(2,1)S(1)}, u32[]{:S(2)}) copy-start(bf16[128,2048]{1,0:T(8,128)(2,1)S(1)} %collective-permute-done.4.refs_6_) | copy-start | bytes 1572868
  109.7 12.2 %collective-permute-start.27 = (bf16[32,4096]{1,0:T(8,128)(2,1)S(1)}, bf16[32,4096]{1,0:T(8,128)(2,1)}, u32[]{:S(2)}, u32[]{:S(2)}) collective-permute-start(bf16[32,4096]{1,0:T(8,128)(2,1)S(1)} %collective-permute-done.19.refs_4_), channel_id=1, source_target_pairs={{0,1},{1,0},{2,3},{3,2},{4,5},{5,4},{6,7},{7,6},{8,9},{9,8},{10,11... | collective-permute-start | bytes 786440 | tf_op jit(solution)/shard_map/ppermute | solution.py:142
  114.9 20.1 %copy-start.11 = (bf16[128,2048]{1,0:T(8,128)(2,1)}, bf16[128,2048]{1,0:T(8,128)(2,1)S(1)}, u32[]{:S(2)}) copy-start(bf16[128,2048]{1,0:T(8,128)(2,1)S(1)} %collective-permute-done.5.refs_7_) | copy-start | bytes 1572868
  114.9 7.8 %collective-permute-start.30 = (bf16[32,4096]{1,0:T(8,128)(2,1)S(1)}, bf16[32,4096]{1,0:T(8,128)(2,1)S(1)}, u32[]{:S(2)}, u32[]{:S(2)}) collective-permute-start(bf16[32,4096]{1,0:T(8,128)(2,1)S(1)} %collective-permute-done.22.refs_7_), channel_id=1, source_target_pairs={{0,1},{1,0},{2,3},{3,2},{4,5},{5,4},{6,7},{7,6},{8,9},{9,8},{10,11... | collective-permute-start | bytes 786440 | tf_op jit(solution)/shard_map/ppermute | solution.py:142
  119.1 9.2 %collective-permute-start.21 = (bf16[32,4096]{1,0:T(8,128)(2,1)}, bf16[32,4096]{1,0:T(8,128)(2,1)S(1)}, u32[]{:S(2)}, u32[]{:S(2)}) collective-permute-start(bf16[32,4096]{1,0:T(8,128)(2,1)} %collective-permute-done.20.refs_5_), channel_id=1, source_target_pairs={{0,2},{1,3},{2,4},{3,5},{4,6},{5,7},{6,8},{7,9},{8,10},{9,11},{10,... | collective-permute-start | bytes 786440 | tf_op jit(solution)/shard_map/ppermute | solution.py:142
  119.1 10.1 %collective-permute-start.24 = (bf16[32,4096]{1,0:T(8,128)(2,1)}, bf16[32,4096]{1,0:T(8,128)(2,1)}, u32[]{:S(2)}, u32[]{:S(2)}) collective-permute-start(bf16[32,4096]{1,0:T(8,128)(2,1)} %collective-permute-done.23.refs_8_), channel_id=1, source_target_pairs={{0,62},{1,63},{2,0},{3,1},{4,2},{5,3},{6,4},{7,5},{8,6},{9,7},{10,... | collective-permute-start | bytes 786440 | tf_op jit(solution)/shard_map/ppermute | solution.py:142
  121.9 11.5 %collective-permute-start = (bf16[128,4096]{1,0:T(8,128)(2,1)S(1)}, bf16[128,4096]{1,0:T(8,128)(2,1)S(1)}, u32[]{:S(2)}, u32[]{:S(2)}) collective-permute-start(bf16[128,4096]{1,0:T(8,128)(2,1)S(1)} %copy-done), channel_id=1, source_target_pairs={{0,1},{1,0},{2,3},{3,2},{4,5},{5,4},{6,7},{7,6},{8,9},{9,8},{10,11... | collective-permute-start | bytes 3145736 | tf_op jit(solution)/shard_map/ppermute | solution.py:142
  122.7 10.7 %collective-permute-start.7 = (bf16[128,4096]{1,0:T(8,128)(2,1)S(1)}, bf16[128,4096]{1,0:T(8,128)(2,1)S(1)}, u32[]{:S(2)}, u32[]{:S(2)}) collective-permute-start(bf16[128,4096]{1,0:T(8,128)(2,1)S(1)} %copy-done.1), channel_id=1, source_target_pairs={{0,1},{1,0},{2,3},{3,2},{4,5},{5,4},{6,7},{7,6},{8,9},{9,8},{10,11... | collective-permute-start | bytes 3145736 | tf_op jit(solution)/shard_map/ppermute | solution.py:142
  128.2 20.1 %copy-start.13 = (bf16[32,4096]{1,0:T(8,128)(2,1)}, bf16[32,4096]{1,0:T(8,128)(2,1)S(1)}, u32[]{:S(2)}) copy-start(bf16[32,4096]{1,0:T(8,128)(2,1)S(1)} %collective-permute-done.21.refs_6_) | copy-start | bytes 786436
  128.2 2.5 %collective-permute-start.16 = (bf16[128,2048]{1,0:T(8,128)(2,1)S(1)}, bf16[128,2048]{1,0:T(8,128)(2,1)S(1)}, u32[]{:S(2)}, u32[]{:S(2)}) collective-permute-start(bf16[128,2048]{1,0:T(8,128)(2,1)S(1)} %broadcast_select_fusion), channel_id=1, source_target_pairs={{0,1},{1,0},{2,3},{3,2},{4,5},{5,4},{6,7},{7,6},{8,9},{9,8},{10,11... | collective-permute-start | bytes 1572872 | tf_op jit(solution)/shard_map/ppermute | solution.py:142
  129.2 5.6 %collective-permute-start.10 = (bf16[128,2048]{1,0:T(8,128)(2,1)S(1)}, bf16[128,2048]{1,0:T(8,128)(2,1)S(1)}, u32[]{:S(2)}, u32[]{:S(2)}) collective-permute-start(bf16[128,2048]{1,0:T(8,128)(2,1)S(1)} %broadcast_select_fusion.2), channel_id=1, source_target_pairs={{0,1},{1,0},{2,3},{3,2},{4,5},{5,4},{6,7},{7,6},{8,9},{9,8},{10,11... | collective-permute-start | bytes 1572872 | tf_op jit(solution)/shard_map/ppermute | solution.py:142
  129.4 5.7 %collective-permute-start.6 = (bf16[128,2048]{1,0:T(8,128)(2,1)S(1)}, bf16[128,2048]{1,0:T(8,128)(2,1)S(1)}, u32[]{:S(2)}, u32[]{:S(2)}) collective-permute-start(bf16[128,2048]{1,0:T(8,128)(2,1)S(1)} %broadcast_select_fusion.3), channel_id=1, source_target_pairs={{0,1},{1,0},{2,3},{3,2},{4,5},{5,4},{6,7},{7,6},{8,9},{9,8},{10,11... | collective-permute-start | bytes 1572872 | tf_op jit(solution)/shard_map/ppermute | solution.py:142
  130.8 5.9 %collective-permute-start.25 = (bf16[32,4096]{1,0:T(8,128)(2,1)S(1)}, bf16[32,4096]{1,0:T(8,128)(2,1)}, u32[]{:S(2)}, u32[]{:S(2)}) collective-permute-start(bf16[32,4096]{1,0:T(8,128)(2,1)S(1)} %broadcast_select_fusion.4), channel_id=1, source_target_pairs={{0,2},{2,4},{4,6},{6,8},{8,10},{10,12},{12,14},{14,16},{16,18},{18... | collective-permute-start | bytes 786440 | tf_op jit(solution)/shard_map/ppermute | solution.py:142
  133.3 23.0 %collective-permute-start.28 = (bf16[32,4096]{1,0:T(8,128)(2,1)}, bf16[32,4096]{1,0:T(8,128)(2,1)S(1)}, u32[]{:S(2)}, u32[]{:S(2)}) collective-permute-start(bf16[32,4096]{1,0:T(8,128)(2,1)} %collective-permute-done.20.refs_5_), channel_id=1, source_target_pairs={{0,1},{1,0},{2,3},{3,2},{4,5},{5,4},{6,7},{7,6},{8,9},{9,8},{10,11... | collective-permute-start | bytes 786440 | tf_op jit(solution)/shard_map/ppermute | solution.py:142
  134.4 22.0 %collective-permute-start.31 = (bf16[32,4096]{1,0:T(8,128)(2,1)}, bf16[32,4096]{1,0:T(8,128)(2,1)S(1)}, u32[]{:S(2)}, u32[]{:S(2)}) collective-permute-start(bf16[32,4096]{1,0:T(8,128)(2,1)} %collective-permute-done.23.refs_8_), channel_id=1, source_target_pairs={{0,1},{1,0},{2,3},{3,2},{4,5},{5,4},{6,7},{7,6},{8,9},{9,8},{10,11... | collective-permute-start | bytes 786440 | tf_op jit(solution)/shard_map/ppermute | solution.py:142
  134.8 21.5 %collective-permute-start.29 = (bf16[32,4096]{1,0:T(8,128)(2,1)S(1)}, bf16[32,4096]{1,0:T(8,128)(2,1)S(1)}, u32[]{:S(2)}, u32[]{:S(2)}) collective-permute-start(bf16[32,4096]{1,0:T(8,128)(2,1)S(1)} %collective-permute-done.21.refs_6_), channel_id=1, source_target_pairs={{0,1},{1,0},{2,3},{3,2},{4,5},{5,4},{6,7},{7,6},{8,9},{9,8},{10,11... | collective-permute-start | bytes 786440 | tf_op jit(solution)/shard_map/ppermute | solution.py:142
  135.0 21.4 %collective-permute-start.32 = (bf16[32,4096]{1,0:T(8,128)(2,1)}, bf16[32,4096]{1,0:T(8,128)(2,1)S(1)}, u32[]{:S(2)}, u32[]{:S(2)}) collective-permute-start(bf16[32,4096]{1,0:T(8,128)(2,1)} %collective-permute-done.24.refs_9_), channel_id=1, source_target_pairs={{0,1},{1,0},{2,3},{3,2},{4,5},{5,4},{6,7},{7,6},{8,9},{9,8},{10,11... | collective-permute-start | bytes 786440 | tf_op jit(solution)/shard_map/ppermute | solution.py:142
  136.7 19.8 %collective-permute-start.33 = (bf16[32,4096]{1,0:T(8,128)(2,1)}, bf16[32,4096]{1,0:T(8,128)(2,1)S(1)}, u32[]{:S(2)}, u32[]{:S(2)}) collective-permute-start(bf16[32,4096]{1,0:T(8,128)(2,1)} %collective-permute-done.25.refs_10_), channel_id=1, source_target_pairs={{0,1},{1,0},{2,3},{3,2},{4,5},{5,4},{6,7},{7,6},{8,9},{9,8},{10,11... | collective-permute-start | bytes 786440 | tf_op jit(solution)/shard_map/ppermute | solution.py:142
  (13 other events, 44.5 us)
where the time goes:
time: 165 us; the launch traced here: 164 us
  starting transfers between devices  92.4 us (56%)
  waiting for transfers between devices  40.3 us (24%)
  Pallas kernels  22.6 us (14%)
  local copies, waits for them, and re-layouts  4.85 us (3%)
  other arithmetic  2.73 us (2%)
    ppermute x34, starting transfers between devices, send(): return lax.ppermute(block, 'tile', route)  92.4 us
    ppermute x34, waiting for transfers between devices, send(): return lax.ppermute(block, 'tile', route)  40.3 us
    pallas_call x2, Pallas kernels, self_attention(): pl.pallas_call(lambda *refs: self_kernel(*refs, head_dim=whole // HEADS),...  16.1 us
    pallas_call x1, Pallas kernels, cross_attention(): pl.pallas_call(lambda *refs: cross_kernel(*refs, head_dim=width // HEADS)...  6.53 us
  transfers between devices with their start and end apart: 34, of which 10 were waited for; matrix products, arithmetic and copies ran while one was open for 3% of the time, Pallas kernels for 10%

commit v1 on v0

--- a/solution.py
+++ b/solution.py
@@ -10,10 +10,7 @@
 HEADS = 32
 LOG2E = 1.4426950408889634
 SELF_FEATURES = 1024
-FEATURES = 1024
-KEY_PARTS = 2
-VALUE_PARTS = 2
-CALLS = 2
+FEATURES = 2048
 
 
 def scores_of(queries, keys):
@@ -29,11 +26,18 @@
     steps = lax.broadcasted_iota(jnp.int32, gate_ref.shape, 0)
     gates = jnp.where(steps == step_ref[0], gate_ref[...].astype(jnp.float32), 0.0)
     gates = jnp.sum(gates, axis=0, keepdims=True)
-    for head in range(query_ref.shape[1] // head_dim):
+
+    def columns(refs, head):
         cols = slice(head * head_dim, (head + 1) * head_dim)
-        keys = jnp.concatenate([ref[:, cols] for ref in key_refs], axis=0)
-        values = jnp.concatenate([ref[:, cols] for ref in value_refs], axis=0)
-        scores = scores_of(query_ref[:, cols], keys)
+        return jnp.concatenate([ref[:, cols] for ref in refs], axis=0)
+
+    heads = query_ref.shape[1] // head_dim
+    ahead = scores_of(columns([query_ref], 0), columns(key_refs, 0))
+    for head in range(heads):
+        scores = ahead
+        if head + 1 < heads:
+            ahead = scores_of(columns([query_ref], head + 1), columns(key_refs, head + 1))
+        cols = slice(head * head_dim, (head + 1) * head_dim)
         scores = jnp.concatenate(
             [scores[:, : 2 * rows]]
             + [scores[:, k * rows : (k + 1) * rows] + bias_ref[k - 2] for k in range(2, 5)],
@@ -43,7 +47,9 @@
         weights = jnp.exp2(scores * scale - top)
         total = jnp.sum(weights, axis=1, keepdims=True)
         summed = jnp.dot(
-            weights.astype(jnp.bfloat16), values, preferred_element_type=jnp.float32
+            weights.astype(jnp.bfloat16),
+            columns(value_refs, head),
+            preferred_element_type=jnp.float32,
         )
         out_ref[:, cols] = summed * (1.0 / total) * gates[:, cols]
 
@@ -72,9 +78,14 @@
         fill(theirs, mine)
 
     scale = LOG2E / math.sqrt(head_dim)
-    for head in range(query_ref.shape[1] // head_dim):
+    heads = query_ref.shape[1] // head_dim
+    ahead = scores_of(query_ref[:, :head_dim], key_buf[:, :head_dim])
+    for head in range(heads):
         cols = slice(head * head_dim, (head + 1) * head_dim)
-        scores = scores_of(query_ref[:, cols], key_buf[:, cols])
+        scores = ahead
+        if head + 1 < heads:
+            after = slice((head + 1) * head_dim, (head + 2) * head_dim)
+            ahead = scores_of(query_ref[:, after], key_buf[:, after])
         top = jnp.max(scores, axis=1, keepdims=True) * scale
         weights = jnp.exp2(scores * scale - top)
         total = jnp.sum(weights, axis=1, keepdims=True)
@@ -86,11 +97,11 @@
 
 def self_attention(bias, timestep, gates, queries, keys, values, first, width, partial):
     rows, whole = queries.shape
-    features = min(SELF_FEATURES, width)
+    features = min(SELF_FEATURES, width // 2)
     offset = first // features
 
     def block_of(array):
-        skip = first % array.shape[1] // features
+        skip = offset if array.shape[1] == whole else 0
         return pl.BlockSpec((array.shape[0], features), lambda i: (0, i + skip))
 
     arrays = (gates, queries, *keys, *values)
@@ -177,34 +188,33 @@
     step = jnp.where(first, -1, 1)
     position = jnp.stack([place - 2, place + 2, place + step])
     bias = jnp.where((position >= 0) & (position < tiles), 0.0, -1e30).astype(jnp.float32)
-
-    def window_of(array, parts):
-        span = width // parts
+    bounds = (0, width // 2, width)
+
+    def window_of(array):
         pieces = []
-        for part in range(parts):
+        for part, (start, end) in enumerate(zip(bounds, bounds[1:])):
             if part > 0:
                 array, _ = lax.optimization_barrier((array, block_below))
-            piece = lax.slice_in_dim(array, part * span, (part + 1) * span, axis=1)
+            piece = lax.slice_in_dim(array, start, end, axis=1)
             below = in_window(piece, 2)
             above = in_window(piece, -2)
             following = partner(jnp.where(first, above, below))
             pieces.append((below, above, following))
         return pieces
 
-    keys = window_of(self_key, KEY_PARTS)
-    values = window_of(self_value, VALUE_PARTS)
+    keys = window_of(self_key)
+    values = window_of(self_value)
     self_part = None
-    share = width // CALLS
-    for call in range(CALLS):
+    for part, (start, end) in enumerate(zip(bounds, bounds[1:])):
         self_part = self_attention(
             bias,
             timestep,
             gate_table,
             self_query,
-            (self_key, key_partner, *keys[call * KEY_PARTS // CALLS]),
-            (self_value, value_partner, *values[call * VALUE_PARTS // CALLS]),
-            call * share,
-            share,
+            (self_key, key_partner, *keys[part]),
+            (self_value, value_partner, *values[part]),
+            start,
+            end - start,
             self_part,
         )
     return cross_attention(core[None], cross_query, self_part, pieces, their_pieces)

time: 165 us -> 159 us (0.964)
  Pallas kernels: 22.6 us -> 17.2 us
    pallas_call x2, Pallas kernels: 16.1 us -> 12.1 us  [self_attention(): pl.pallas_call(lambda *refs: self_kernel(*refs, head_dim=whole // HEADS),...]
  transfers between devices with their start and end apart: 34 -> 34, of which waited for: 10 -> 10; matrix products, arithmetic and copies ran while one was open for 3% -> 3% of each run, Pallas kernels for 10% -> 8%
where the time goes in v1:
time: 159 us
  starting transfers between devices  92.4 us (58%)
  waiting for transfers between devices  40.3 us (25%)
  Pallas kernels  17.2 us (11%)
  local copies, waits for them, and re-layouts  4.85 us (3%)
  other arithmetic  2.73 us (2%)
    ppermute x34, starting transfers between devices, send(): return lax.ppermute(block, 'tile', route)  92.4 us
    ppermute x34, waiting for transfers between devices, send(): return lax.ppermute(block, 'tile', route)  40.3 us
    pallas_call x2, Pallas kernels, self_attention(): pl.pallas_call(lambda *refs: self_kernel(*refs, head_dim=whole // HEADS),...  12.1 us
    pallas_call x1, Pallas kernels, cross_attention(): pl.pallas_call(lambda *refs: cross_kernel(*refs, head_dim=width // HEADS)...  5.1 us
  transfers between devices with their start and end apart: 34, of which 10 were waited for; matrix products, arithmetic and copies ran while one was open for 3% of the time, Pallas kernels for 8%

profile of v1, /device:TPU:37, one launch (start us, length us, event | category | flops | bytes accessed | tf_op | source)
XLA Modules:
  0.0 158.7 jit_solution(18049008249844930389)
XLA Ops:
  0.0 20.4 %collective-permute-start.1 = (bf16[4,4096]{1,0:T(4,128)(2,1)}, bf16[4,4096]{1,0:T(4,128)(2,1)S(1)}, u32[]{:S(2)}, u32[]{:S(2)}) collective-permute-start(bf16[4,4096]{1,0:T(4,128)(2,1)} %param.12), channel_id=1, source_target_pairs={{0,1},{1,0},{2,3},{3,2},{4,5},{5,4},{6,7},{7,6},{8,9},{9,8},{10,11... | collective-permute-start | bytes 98312 | tf_op jit(solution)/shard_map/ppermute | solution.py:153
  20.4 1.1 collective-permute-done.1
  21.5 0.3 collective-permute-done.2
  21.8 0.8 maximum_select_fusion
  22.8 10.2 %collective-permute-start.17 = (bf16[8,4096]{1,0:T(8,128)(2,1)S(1)}, bf16[8,4096]{1,0:T(8,128)(2,1)S(1)}, u32[]{:S(2)}, u32[]{:S(2)}) collective-permute-start(bf16[8,4096]{1,0:T(8,128)(2,1)S(1)} %maximum_select_fusion), channel_id=1, source_target_pairs={{0,48},{1,49},{2,50},{3,51},{4,52},{5,53},{6,54},{7,55},{8,56},{9,... | collective-permute-start | bytes 196616 | tf_op jit(solution)/shard_map/ppermute | solution.py:153
  33.0 2.0 %collective-permute-done.3 = bf16[8,4096]{1,0:T(8,128)(2,1)S(1)} collective-permute-done((bf16[8,4096]{1,0:T(8,128)(2,1)S(1)}, bf16[8,4096]{1,0:T(8,128)(2,1)S(1)}, u32[]{:S(2)}, u32[]{:S(2)}) %collective-permute-start.3) | collective-permute-done | bytes 65568 | tf_op jit(solution)/shard_map/ppermute | solution.py:153
  35.0 10.4 %collective-permute-done.17 = bf16[8,4096]{1,0:T(8,128)(2,1)S(1)} collective-permute-done((bf16[8,4096]{1,0:T(8,128)(2,1)S(1)}, bf16[8,4096]{1,0:T(8,128)(2,1)S(1)}, u32[]{:S(2)}, u32[]{:S(2)}) %collective-permute-start.17) | collective-permute-done | bytes 65568 | tf_op jit(solution)/shard_map/ppermute | solution.py:153
  45.4 4.6 %collective-permute-start.18 = (bf16[8,4096]{1,0:T(8,128)(2,1)S(1)}, bf16[8,4096]{1,0:T(8,128)(2,1)S(1)}, u32[]{:S(2)}, u32[]{:S(2)}) collective-permute-start(bf16[8,4096]{1,0:T(8,128)(2,1)S(1)} %broadcast_select_fusion.5), channel_id=1, source_target_pairs={{0,16},{2,18},{4,20},{6,22},{8,24},{10,26},{12,28},{14,30},{16,32}... | collective-permute-start | bytes 196616 | tf_op jit(solution)/shard_map/ppermute | solution.py:153
  50.0 1.1 slice.14
  51.1 3.6 %collective-permute-start.11 = (bf16[128,2048]{1,0:T(8,128)(2,1)S(1)}, bf16[128,2048]{1,0:T(8,128)(2,1)S(1)}, u32[]{:S(2)}, u32[]{:S(2)}) collective-permute-start(bf16[128,2048]{1,0:T(8,128)(2,1)S(1)} %slice.14), channel_id=1, source_target_pairs={{0,2},{1,3},{2,4},{3,5},{4,6},{5,7},{6,8},{7,9},{8,10},{9,11},{10,... | collective-permute-start | bytes 1572872 | tf_op jit(solution)/shard_map/ppermute | solution.py:153
  54.7 1.3 collective-permute-start.12
  56.0 1.8 %collective-permute-done.18 = bf16[8,4096]{1,0:T(8,128)(2,1)S(1)} collective-permute-done((bf16[8,4096]{1,0:T(8,128)(2,1)S(1)}, bf16[8,4096]{1,0:T(8,128)(2,1)S(1)}, u32[]{:S(2)}, u32[]{:S(2)}) %collective-permute-start.18) | collective-permute-done | bytes 65568 | tf_op jit(solution)/shard_map/ppermute | solution.py:153
  57.8 1.1 collective-permute-start.19
  59.0 1.1 slice.15
  60.0 3.3 %collective-permute-start.14 = (bf16[128,2048]{1,0:T(8,128)(2,1)S(1)}, bf16[128,2048]{1,0:T(8,128)(2,1)S(1)}, u32[]{:S(2)}, u32[]{:S(2)}) collective-permute-start(bf16[128,2048]{1,0:T(8,128)(2,1)S(1)} %slice.15), channel_id=1, source_target_pairs={{0,2},{1,3},{2,4},{3,5},{4,6},{5,7},{6,8},{7,9},{8,10},{9,11},{10,... | collective-permute-start | bytes 1572872 | tf_op jit(solution)/shard_map/ppermute | solution.py:153
  63.3 1.3 collective-permute-start.15
  64.7 6.4 %collective-permute-done.19.refs_4_ = bf16[32,4096]{1,0:T(8,128)(2,1)S(1)} collective-permute-done((bf16[32,4096]{1,0:T(8,128)(2,1)S(1)}, bf16[32,4096]{1,0:T(8,128)(2,1)S(1)}, u32[]{:S(2)}, u32[]{:S(2)}) %collective-permute-start.19) | collective-permute-done | bytes 262176 | tf_op jit(solution)/shard_map/ppermute | solution.py:153
  71.2 4.2 %collective-permute-start.8 = (bf16[128,2048]{1,0:T(8,128)(2,1)S(1)}, bf16[128,2048]{1,0:T(8,128)(2,1)S(1)}, u32[]{:S(2)}, u32[]{:S(2)}) collective-permute-start(bf16[128,2048]{1,0:T(8,128)(2,1)S(1)} %slice.13), channel_id=1, source_target_pairs={{0,2},{1,3},{2,4},{3,5},{4,6},{5,7},{6,8},{7,9},{8,10},{9,11},{10,... | collective-permute-start | bytes 1572872 | tf_op jit(solution)/shard_map/ppermute | solution.py:153
  75.4 1.3 collective-permute-start.9
  76.7 7.9 %collective-permute-start.22 = (bf16[32,4096]{1,0:T(8,128)(2,1)S(1)}, bf16[32,4096]{1,0:T(8,128)(2,1)S(1)}, u32[]{:S(2)}, u32[]{:S(2)}) collective-permute-start(bf16[32,4096]{1,0:T(8,128)(2,1)S(1)} %pad_maximum_fusion.refs_3_), channel_id=1, source_target_pairs={{0,62},{1,63},{2,0},{3,1},{4,2},{5,3},{6,4},{7,5},{8,6},{9,7},{10,... | collective-permute-start | bytes 786440 | tf_op jit(solution)/shard_map/ppermute | solution.py:153
  84.7 11.2 %collective-permute-done.22.refs_7_ = bf16[32,4096]{1,0:T(8,128)(2,1)S(1)} collective-permute-done((bf16[32,4096]{1,0:T(8,128)(2,1)S(1)}, bf16[32,4096]{1,0:T(8,128)(2,1)S(1)}, u32[]{:S(2)}, u32[]{:S(2)}) %collective-permute-start.22) | collective-permute-done | bytes 262176 | tf_op jit(solution)/shard_map/ppermute | solution.py:153
  95.9 4.1 %collective-permute-start.4 = (bf16[128,2048]{1,0:T(8,128)(2,1)S(1)}, bf16[128,2048]{1,0:T(8,128)(2,1)S(1)}, u32[]{:S(2)}, u32[]{:S(2)}) collective-permute-start(bf16[128,2048]{1,0:T(8,128)(2,1)S(1)} %slice.12), channel_id=1, source_target_pairs={{0,2},{1,3},{2,4},{3,5},{4,6},{5,7},{6,8},{7,9},{8,10},{9,11},{10,... | collective-permute-start | bytes 1572872 | tf_op jit(solution)/shard_map/ppermute | solution.py:153
  100.0 1.3 collective-permute-start.5
  101.3 3.4 %collective-permute-start.26 = (bf16[32,4096]{1,0:T(8,128)(2,1)S(1)}, bf16[32,4096]{1,0:T(8,128)(2,1)S(1)}, u32[]{:S(2)}, u32[]{:S(2)}) collective-permute-start(bf16[32,4096]{1,0:T(8,128)(2,1)S(1)} %pad_maximum_fusion.refs_3_), channel_id=1, source_target_pairs={{0,1},{1,0},{2,3},{3,2},{4,5},{5,4},{6,7},{7,6},{8,9},{9,8},{10,11... | collective-permute-start | bytes 786440 | tf_op jit(solution)/shard_map/ppermute | solution.py:153
  104.8 1.1 collective-permute-done.26.refs_11_
  105.9 2.4 %collective-permute-start.20 = (bf16[32,4096]{1,0:T(8,128)(2,1)S(1)}, bf16[32,4096]{1,0:T(8,128)(2,1)}, u32[]{:S(2)}, u32[]{:S(2)}) collective-permute-start(bf16[32,4096]{1,0:T(8,128)(2,1)S(1)} %collective-permute-done.19.refs_4_), channel_id=1, source_target_pairs={{0,2},{1,3},{2,4},{3,5},{4,6},{5,7},{6,8},{7,9},{8,10},{9,11},{10,... | collective-permute-start | bytes 786440 | tf_op jit(solution)/shard_map/ppermute | solution.py:153
  108.3 0.3 collective-permute-start.23
  108.6 0.9 collective-permute-start.13
  109.7 5.2 %collective-permute-start.27 = (bf16[32,4096]{1,0:T(8,128)(2,1)S(1)}, bf16[32,4096]{1,0:T(8,128)(2,1)}, u32[]{:S(2)}, u32[]{:S(2)}) collective-permute-start(bf16[32,4096]{1,0:T(8,128)(2,1)S(1)} %collective-permute-done.19.refs_4_), channel_id=1, source_target_pairs={{0,1},{1,0},{2,3},{3,2},{4,5},{5,4},{6,7},{7,6},{8,9},{9,8},{10,11... | collective-permute-start | bytes 786440 | tf_op jit(solution)/shard_map/ppermute | solution.py:153
  114.9 4.2 %collective-permute-start.30 = (bf16[32,4096]{1,0:T(8,128)(2,1)S(1)}, bf16[32,4096]{1,0:T(8,128)(2,1)S(1)}, u32[]{:S(2)}, u32[]{:S(2)}) collective-permute-start(bf16[32,4096]{1,0:T(8,128)(2,1)S(1)} %collective-permute-done.22.refs_7_), channel_id=1, source_target_pairs={{0,1},{1,0},{2,3},{3,2},{4,5},{5,4},{6,7},{7,6},{8,9},{9,8},{10,11... | collective-permute-start | bytes 786440 | tf_op jit(solution)/shard_map/ppermute | solution.py:153
  119.1 2.7 %collective-permute-start.24 = (bf16[32,4096]{1,0:T(8,128)(2,1)}, bf16[32,4096]{1,0:T(8,128)(2,1)}, u32[]{:S(2)}, u32[]{:S(2)}) collective-permute-start(bf16[32,4096]{1,0:T(8,128)(2,1)} %collective-permute-done.23.refs_8_), channel_id=1, source_target_pairs={{0,62},{1,63},{2,0},{3,1},{4,2},{5,3},{6,4},{7,5},{8,6},{9,7},{10,... | collective-permute-start | bytes 786440 | tf_op jit(solution)/shard_map/ppermute | solution.py:153
  121.9 0.8 collective-permute-start
  122.8 0.5 copy-done.21
  123.4 4.9 %collective-permute-done.21.refs_6_ = bf16[32,4096]{1,0:T(8,128)(2,1)S(1)} collective-permute-done((bf16[32,4096]{1,0:T(8,128)(2,1)}, bf16[32,4096]{1,0:T(8,128)(2,1)S(1)}, u32[]{:S(2)}, u32[]{:S(2)}) %collective-permute-start.21) | collective-permute-done | bytes 262176 | tf_op jit(solution)/shard_map/ppermute | solution.py:153
  128.2 1.0 collective-permute-start.16
  129.4 0.4 collective-permute-start.6
  129.7 1.0 broadcast_select_fusion.4
  130.8 2.6 %collective-permute-start.25 = (bf16[32,4096]{1,0:T(8,128)(2,1)S(1)}, bf16[32,4096]{1,0:T(8,128)(2,1)}, u32[]{:S(2)}, u32[]{:S(2)}) collective-permute-start(bf16[32,4096]{1,0:T(8,128)(2,1)S(1)} %broadcast_select_fusion.4), channel_id=1, source_target_pairs={{0,2},{2,4},{4,6},{6,8},{8,10},{10,12},{12,14},{14,16},{16,18},{18... | collective-permute-start | bytes 786440 | tf_op jit(solution)/shard_map/ppermute | solution.py:153
  133.4 1.0 copy-done.3
  134.4 0.5 collective-permute-start.31
  135.0 0.6 collective-permute-start.32
  135.6 1.0 collective-permute-done.25.refs_10_
  136.7 2.3 %collective-permute-start.33 = (bf16[32,4096]{1,0:T(8,128)(2,1)}, bf16[32,4096]{1,0:T(8,128)(2,1)S(1)}, u32[]{:S(2)}, u32[]{:S(2)}) collective-permute-start(bf16[32,4096]{1,0:T(8,128)(2,1)} %collective-permute-done.25.refs_10_), channel_id=1, source_target_pairs={{0,1},{1,0},{2,3},{3,2},{4,5},{5,4},{6,7},{7,6},{8,9},{9,8},{10,11... | collective-permute-start | bytes 786440 | tf_op jit(solution)/shard_map/ppermute | solution.py:153
  139.6 0.7 and_select_fusion.refs_0_
  140.3 6.0 %self_attention.2.refs_14_ = f32[128,4096]{1,0:T(8,128)} custom-call(f32[3]{0:T(128)} %and_select_fusion.refs_0_, s32[1]{0:T(128)S(6)} %copy.11.refs_1_, bf16[50,4096]{1,0:T(8,128)(2,1)} %refs_2_.3, bf16[128,4096]{1,0:T(8,128)(2,1)} %refs_3_.3, bf16[128,4096]{1,0:T(8,128)(2,1)} %refs_4_.3, bf16[128,4096]{1,0:T(8,128)(2,1)} %copy-done.2, ...), custom_call_target="tpu_custom_call" | custom-call | tf_op jit(solution)/shard_map/self_attention/pallas_call | solution.py:114
  146.3 6.0 %self_attention.3.refs_2_ = f32[128,4096]{1,0:T(8,128)} custom-call(f32[3]{0:T(128)} %and_select_fusion.refs_0_, s32[1]{0:T(128)S(6)} %copy.11.refs_1_, bf16[50,4096]{1,0:T(8,128)(2,1)} %refs_2_.3, bf16[128,4096]{1,0:T(8,128)(2,1)} %refs_3_.3, bf16[128,4096]{1,0:T(8,128)(2,1)} %refs_4_.3, ...), custom_call_target="tpu_custom_call", output_to_operand_aliasing={{}: (14, {})} | custom-call | tf_op jit(solution)/shard_map/self_attention/pallas_call | solution.py:114
  152.5 0.6 copy-done.22
  153.4 5.1 %cross_attention.1 = bf16[128,4096]{1,0:T(8,128)(2,1)} custom-call(s32[1]{0:T(128)} %bitcast.refs_0_, bf16[128,4096]{1,0:T(8,128)(2,1)} %refs_1_.3, f32[128,4096]{1,0:T(8,128)} %self_attention.3.refs_2_, bf16[32,4096]{1,0:T(8,128)(2,1)} %copy-done.12, bf16[32,4096]{1,0:T(8,128)(2,1)} %copy-done.18, bf16[32,4096]{1,0:T(8,128)(2,1)} %collective-permute-done.20.refs_5_, ...), custom_call_target="tpu_custom_call" | custom-call | tf_op jit(solution)/shard_map/cross_attention/pallas_call | solution.py:130
  (90 shorter events, 1.5 us)
Async XLA Ops:
  0.0 64.7 %copy-start = (bf16[128,4096]{1,0:T(8,128)(2,1)S(1)}, bf16[128,4096]{1,0:T(8,128)(2,1)}, u32[]{:S(2)}) copy-start(bf16[128,4096]{1,0:T(8,128)(2,1)} %refs_4_.3) | copy-start | bytes 3145732
  0.0 64.6 %copy-start.1 = (bf16[128,4096]{1,0:T(8,128)(2,1)S(1)}, bf16[128,4096]{1,0:T(8,128)(2,1)}, u32[]{:S(2)}) copy-start(bf16[128,4096]{1,0:T(8,128)(2,1)} %refs_9_.3) | copy-start | bytes 3145732
  0.0 21.5 %collective-permute-start.1 = (bf16[4,4096]{1,0:T(4,128)(2,1)}, bf16[4,4096]{1,0:T(4,128)(2,1)S(1)}, u32[]{:S(2)}, u32[]{:S(2)}) collective-permute-start(bf16[4,4096]{1,0:T(4,128)(2,1)} %param.12), channel_id=1, source_target_pairs={{0,1},{1,0},{2,3},{3,2},{4,5},{5,4},{6,7},{7,6},{8,9},{9,8},{10,11... | collective-permute-start | bytes 98312 | tf_op jit(solution)/shard_map/ppermute | solution.py:153
  20.4 1.4 collective-permute-start.2
  22.7 12.3 %collective-permute-start.3 = (bf16[8,4096]{1,0:T(8,128)(2,1)S(1)}, bf16[8,4096]{1,0:T(8,128)(2,1)S(1)}, u32[]{:S(2)}, u32[]{:S(2)}) collective-permute-start(bf16[8,4096]{1,0:T(8,128)(2,1)S(1)} %maximum_select_fusion), channel_id=1, source_target_pairs={{0,16},{1,17},{2,18},{3,19},{4,20},{5,21},{6,22},{7,23},{8,24},{9,... | collective-permute-start | bytes 196616 | tf_op jit(solution)/shard_map/ppermute | solution.py:153
  22.8 22.6 %collective-permute-start.17 = (bf16[8,4096]{1,0:T(8,128)(2,1)S(1)}, bf16[8,4096]{1,0:T(8,128)(2,1)S(1)}, u32[]{:S(2)}, u32[]{:S(2)}) collective-permute-start(bf16[8,4096]{1,0:T(8,128)(2,1)S(1)} %maximum_select_fusion), channel_id=1, source_target_pairs={{0,48},{1,49},{2,50},{3,51},{4,52},{5,53},{6,54},{7,55},{8,56},{9,... | collective-permute-start | bytes 196616 | tf_op jit(solution)/shard_map/ppermute | solution.py:153
  45.4 12.4 %collective-permute-start.18 = (bf16[8,4096]{1,0:T(8,128)(2,1)S(1)}, bf16[8,4096]{1,0:T(8,128)(2,1)S(1)}, u32[]{:S(2)}, u32[]{:S(2)}) collective-permute-start(bf16[8,4096]{1,0:T(8,128)(2,1)S(1)} %broadcast_select_fusion.5), channel_id=1, source_target_pairs={{0,16},{2,18},{4,20},{6,22},{8,24},{10,26},{12,28},{14,30},{16,32}... | collective-permute-start | bytes 196616 | tf_op jit(solution)/shard_map/ppermute | solution.py:153
  51.1 24.3 %collective-permute-start.11 = (bf16[128,2048]{1,0:T(8,128)(2,1)S(1)}, bf16[128,2048]{1,0:T(8,128)(2,1)S(1)}, u32[]{:S(2)}, u32[]{:S(2)}) collective-permute-start(bf16[128,2048]{1,0:T(8,128)(2,1)S(1)} %slice.14), channel_id=1, source_target_pairs={{0,2},{1,3},{2,4},{3,5},{4,6},{5,7},{6,8},{7,9},{8,10},{9,11},{10,... | collective-permute-start | bytes 1572872 | tf_op jit(solution)/shard_map/ppermute | solution.py:153
  54.7 21.9 %collective-permute-start.12 = (bf16[128,2048]{1,0:T(8,128)(2,1)S(1)}, bf16[128,2048]{1,0:T(8,128)(2,1)S(1)}, u32[]{:S(2)}, u32[]{:S(2)}) collective-permute-start(bf16[128,2048]{1,0:T(8,128)(2,1)S(1)} %slice.14), channel_id=1, source_target_pairs={{2,0},{3,1},{4,2},{5,3},{6,4},{7,5},{8,6},{9,7},{10,8},{11,9},{12,... | collective-permute-start | bytes 1572872 | tf_op jit(solution)/shard_map/ppermute | solution.py:153
  57.8 43.5 %copy-start.12 = (bf16[32,4096]{1,0:T(8,128)(2,1)}, bf16[32,4096]{1,0:T(8,128)(2,1)S(1)}, u32[]{:S(2)}) copy-start(bf16[32,4096]{1,0:T(8,128)(2,1)S(1)} %pad_maximum_fusion.refs_3_) | copy-start | bytes 786436
  57.8 13.3 %collective-permute-start.19 = (bf16[32,4096]{1,0:T(8,128)(2,1)S(1)}, bf16[32,4096]{1,0:T(8,128)(2,1)S(1)}, u32[]{:S(2)}, u32[]{:S(2)}) collective-permute-start(bf16[32,4096]{1,0:T(8,128)(2,1)S(1)} %pad_maximum_fusion.refs_3_), channel_id=1, source_target_pairs={{0,2},{1,3},{2,4},{3,5},{4,6},{5,7},{6,8},{7,9},{8,10},{9,11},{10,... | collective-permute-start | bytes 786440 | tf_op jit(solution)/shard_map/ppermute | solution.py:153
  60.0 40.0 %collective-permute-start.14 = (bf16[128,2048]{1,0:T(8,128)(2,1)S(1)}, bf16[128,2048]{1,0:T(8,128)(2,1)S(1)}, u32[]{:S(2)}, u32[]{:S(2)}) collective-permute-start(bf16[128,2048]{1,0:T(8,128)(2,1)S(1)} %slice.15), channel_id=1, source_target_pairs={{0,2},{1,3},{2,4},{3,5},{4,6},{5,7},{6,8},{7,9},{8,10},{9,11},{10,... | collective-permute-start | bytes 1572872 | tf_op jit(solution)/shard_map/ppermute | solution.py:153
  63.3 38.0 %collective-permute-start.15 = (bf16[128,2048]{1,0:T(8,128)(2,1)S(1)}, bf16[128,2048]{1,0:T(8,128)(2,1)S(1)}, u32[]{:S(2)}, u32[]{:S(2)}) collective-permute-start(bf16[128,2048]{1,0:T(8,128)(2,1)S(1)} %slice.15), channel_id=1, source_target_pairs={{2,0},{3,1},{4,2},{5,3},{6,4},{7,5},{8,6},{9,7},{10,8},{11,9},{12,... | collective-permute-start | bytes 1572872 | tf_op jit(solution)/shard_map/ppermute | solution.py:153
  71.2 38.5 %copy-start.18 = (bf16[32,4096]{1,0:T(8,128)(2,1)}, bf16[32,4096]{1,0:T(8,128)(2,1)S(1)}, u32[]{:S(2)}) copy-start(bf16[32,4096]{1,0:T(8,128)(2,1)S(1)} %collective-permute-done.19.refs_4_) | copy-start | bytes 786436
  71.2 37.2 %collective-permute-start.8 = (bf16[128,2048]{1,0:T(8,128)(2,1)S(1)}, bf16[128,2048]{1,0:T(8,128)(2,1)S(1)}, u32[]{:S(2)}, u32[]{:S(2)}) collective-permute-start(bf16[128,2048]{1,0:T(8,128)(2,1)S(1)} %slice.13), channel_id=1, source_target_pairs={{0,2},{1,3},{2,4},{3,5},{4,6},{5,7},{6,8},{7,9},{8,10},{9,11},{10,... | collective-permute-start | bytes 1572872 | tf_op jit(solution)/shard_map/ppermute | solution.py:153
  75.3 34.3 %copy-start.4 = (bf16[128,2048]{1,0:T(8,128)(2,1)}, bf16[128,2048]{1,0:T(8,128)(2,1)S(1)}, u32[]{:S(2)}) copy-start(bf16[128,2048]{1,0:T(8,128)(2,1)S(1)} %collective-permute-done.11.refs_6_) | copy-start | bytes 1572868
  75.4 33.3 %collective-permute-start.9 = (bf16[128,2048]{1,0:T(8,128)(2,1)S(1)}, bf16[128,2048]{1,0:T(8,128)(2,1)S(1)}, u32[]{:S(2)}, u32[]{:S(2)}) collective-permute-start(bf16[128,2048]{1,0:T(8,128)(2,1)S(1)} %slice.13), channel_id=1, source_target_pairs={{2,0},{3,1},{4,2},{5,3},{6,4},{7,5},{8,6},{9,7},{10,8},{11,9},{12,... | collective-permute-start | bytes 1572872 | tf_op jit(solution)/shard_map/ppermute | solution.py:153
  76.7 33.0 %copy-start.5 = (bf16[128,2048]{1,0:T(8,128)(2,1)}, bf16[128,2048]{1,0:T(8,128)(2,1)S(1)}, u32[]{:S(2)}) copy-start(bf16[128,2048]{1,0:T(8,128)(2,1)S(1)} %collective-permute-done.12.refs_7_) | copy-start | bytes 1572868
  76.7 19.2 %collective-permute-start.22 = (bf16[32,4096]{1,0:T(8,128)(2,1)S(1)}, bf16[32,4096]{1,0:T(8,128)(2,1)S(1)}, u32[]{:S(2)}, u32[]{:S(2)}) collective-permute-start(bf16[32,4096]{1,0:T(8,128)(2,1)S(1)} %pad_maximum_fusion.refs_3_), channel_id=1, source_target_pairs={{0,62},{1,63},{2,0},{3,1},{4,2},{5,3},{6,4},{7,5},{8,6},{9,7},{10,... | collective-permute-start | bytes 786440 | tf_op jit(solution)/shard_map/ppermute | solution.py:153
  95.9 25.9 %copy-start.19 = (bf16[32,4096]{1,0:T(8,128)(2,1)}, bf16[32,4096]{1,0:T(8,128)(2,1)S(1)}, u32[]{:S(2)}) copy-start(bf16[32,4096]{1,0:T(8,128)(2,1)S(1)} %collective-permute-done.22.refs_7_) | copy-start | bytes 786436
  95.9 13.8 %collective-permute-start.4 = (bf16[128,2048]{1,0:T(8,128)(2,1)S(1)}, bf16[128,2048]{1,0:T(8,128)(2,1)S(1)}, u32[]{:S(2)}, u32[]{:S(2)}) collective-permute-start(bf16[128,2048]{1,0:T(8,128)(2,1)S(1)} %slice.12), channel_id=1, source_target_pairs={{0,2},{1,3},{2,4},{3,5},{4,6},{5,7},{6,8},{7,9},{8,10},{9,11},{10,... | collective-permute-start | bytes 1572872 | tf_op jit(solution)/shard_map/ppermute | solution.py:153
  100.0 21.8 %copy-start.6 = (bf16[128,2048]{1,0:T(8,128)(2,1)}, bf16[128,2048]{1,0:T(8,128)(2,1)S(1)}, u32[]{:S(2)}) copy-start(bf16[128,2048]{1,0:T(8,128)(2,1)S(1)} %collective-permute-done.14.refs_11_) | copy-start | bytes 1572868
  100.0 14.9 %collective-permute-start.5 = (bf16[128,2048]{1,0:T(8,128)(2,1)S(1)}, bf16[128,2048]{1,0:T(8,128)(2,1)S(1)}, u32[]{:S(2)}, u32[]{:S(2)}) collective-permute-start(bf16[128,2048]{1,0:T(8,128)(2,1)S(1)} %slice.12), channel_id=1, source_target_pairs={{2,0},{3,1},{4,2},{5,3},{6,4},{7,5},{8,6},{9,7},{10,8},{11,9},{12,... | collective-permute-start | bytes 1572872 | tf_op jit(solution)/shard_map/ppermute | solution.py:153
  101.3 20.5 %copy-start.7 = (bf16[128,2048]{1,0:T(8,128)(2,1)}, bf16[128,2048]{1,0:T(8,128)(2,1)S(1)}, u32[]{:S(2)}) copy-start(bf16[128,2048]{1,0:T(8,128)(2,1)S(1)} %collective-permute-done.15.refs_12_) | copy-start | bytes 1572868
  101.3 4.6 %collective-permute-start.26 = (bf16[32,4096]{1,0:T(8,128)(2,1)S(1)}, bf16[32,4096]{1,0:T(8,128)(2,1)S(1)}, u32[]{:S(2)}, u32[]{:S(2)}) collective-permute-start(bf16[32,4096]{1,0:T(8,128)(2,1)S(1)} %pad_maximum_fusion.refs_3_), channel_id=1, source_target_pairs={{0,1},{1,0},{2,3},{3,2},{4,5},{5,4},{6,7},{7,6},{8,9},{9,8},{10,11... | collective-permute-start | bytes 786440 | tf_op jit(solution)/shard_map/ppermute | solution.py:153
  105.9 13.1 %collective-permute-start.20 = (bf16[32,4096]{1,0:T(8,128)(2,1)S(1)}, bf16[32,4096]{1,0:T(8,128)(2,1)}, u32[]{:S(2)}, u32[]{:S(2)}) collective-permute-start(bf16[32,4096]{1,0:T(8,128)(2,1)S(1)} %collective-permute-done.19.refs_4_), channel_id=1, source_target_pairs={{0,2},{1,3},{2,4},{3,5},{4,6},{5,7},{6,8},{7,9},{8,10},{9,11},{10,... | collective-permute-start | bytes 786440 | tf_op jit(solution)/shard_map/ppermute | solution.py:153
  108.3 26.5 %copy-start.8 = (bf16[128,2048]{1,0:T(8,128)(2,1)}, bf16[128,2048]{1,0:T(8,128)(2,1)S(1)}, u32[]{:S(2)}) copy-start(bf16[128,2048]{1,0:T(8,128)(2,1)S(1)} %collective-permute-done.8.refs_11_) | copy-start | bytes 1572868
  108.3 10.8 %collective-permute-start.23 = (bf16[32,4096]{1,0:T(8,128)(2,1)S(1)}, bf16[32,4096]{1,0:T(8,128)(2,1)}, u32[]{:S(2)}, u32[]{:S(2)}) collective-permute-start(bf16[32,4096]{1,0:T(8,128)(2,1)S(1)} %collective-permute-done.22.refs_7_), channel_id=1, source_target_pairs={{0,62},{1,63},{2,0},{3,1},{4,2},{5,3},{6,4},{7,5},{8,6},{9,7},{10,... | collective-permute-start | bytes 786440 | tf_op jit(solution)/shard_map/ppermute | solution.py:153
  108.6 26.2 %copy-start.9 = (bf16[128,2048]{1,0:T(8,128)(2,1)}, bf16[128,2048]{1,0:T(8,128)(2,1)S(1)}, u32[]{:S(2)}) copy-start(bf16[128,2048]{1,0:T(8,128)(2,1)S(1)} %collective-permute-done.9.refs_12_) | copy-start | bytes 1572868
  108.6 20.7 %collective-permute-start.13 = (bf16[128,2048]{1,0:T(8,128)(2,1)S(1)}, bf16[128,2048]{1,0:T(8,128)(2,1)S(1)}, u32[]{:S(2)}, u32[]{:S(2)}) collective-permute-start(bf16[128,2048]{1,0:T(8,128)(2,1)S(1)} %broadcast_select_fusion.1), channel_id=1, source_target_pairs={{0,1},{1,0},{2,3},{3,2},{4,5},{5,4},{6,7},{7,6},{8,9},{9,8},{10,11... | collective-permute-start | bytes 1572872 | tf_op jit(solution)/shard_map/ppermute | solution.py:153
  109.7 25.4 %copy-start.10 = (bf16[128,2048]{1,0:T(8,128)(2,1)}, bf16[128,2048]{1,0:T(8,128)(2,1)S(1)}, u32[]{:S(2)}) copy-start(bf16[128,2048]{1,0:T(8,128)(2,1)S(1)} %collective-permute-done.4.refs_6_) | copy-start | bytes 1572868
  109.7 12.2 %collective-permute-start.27 = (bf16[32,4096]{1,0:T(8,128)(2,1)S(1)}, bf16[32,4096]{1,0:T(8,128)(2,1)}, u32[]{:S(2)}, u32[]{:S(2)}) collective-permute-start(bf16[32,4096]{1,0:T(8,128)(2,1)S(1)} %collective-permute-done.19.refs_4_), channel_id=1, source_target_pairs={{0,1},{1,0},{2,3},{3,2},{4,5},{5,4},{6,7},{7,6},{8,9},{9,8},{10,11... | collective-permute-start | bytes 786440 | tf_op jit(solution)/shard_map/ppermute | solution.py:153
  114.9 20.1 %copy-start.11 = (bf16[128,2048]{1,0:T(8,128)(2,1)}, bf16[128,2048]{1,0:T(8,128)(2,1)S(1)}, u32[]{:S(2)}) copy-start(bf16[128,2048]{1,0:T(8,128)(2,1)S(1)} %collective-permute-done.5.refs_7_) | copy-start | bytes 1572868
  114.9 7.8 %collective-permute-start.30 = (bf16[32,4096]{1,0:T(8,128)(2,1)S(1)}, bf16[32,4096]{1,0:T(8,128)(2,1)S(1)}, u32[]{:S(2)}, u32[]{:S(2)}) collective-permute-start(bf16[32,4096]{1,0:T(8,128)(2,1)S(1)} %collective-permute-done.22.refs_7_), channel_id=1, source_target_pairs={{0,1},{1,0},{2,3},{3,2},{4,5},{5,4},{6,7},{7,6},{8,9},{9,8},{10,11... | collective-permute-start | bytes 786440 | tf_op jit(solution)/shard_map/ppermute | solution.py:153
  119.1 9.2 %collective-permute-start.21 = (bf16[32,4096]{1,0:T(8,128)(2,1)}, bf16[32,4096]{1,0:T(8,128)(2,1)S(1)}, u32[]{:S(2)}, u32[]{:S(2)}) collective-permute-start(bf16[32,4096]{1,0:T(8,128)(2,1)} %collective-permute-done.20.refs_5_), channel_id=1, source_target_pairs={{0,2},{1,3},{2,4},{3,5},{4,6},{5,7},{6,8},{7,9},{8,10},{9,11},{10,... | collective-permute-start | bytes 786440 | tf_op jit(solution)/shard_map/ppermute | solution.py:153
  119.1 10.1 %collective-permute-start.24 = (bf16[32,4096]{1,0:T(8,128)(2,1)}, bf16[32,4096]{1,0:T(8,128)(2,1)}, u32[]{:S(2)}, u32[]{:S(2)}) collective-permute-start(bf16[32,4096]{1,0:T(8,128)(2,1)} %collective-permute-done.23.refs_8_), channel_id=1, source_target_pairs={{0,62},{1,63},{2,0},{3,1},{4,2},{5,3},{6,4},{7,5},{8,6},{9,7},{10,... | collective-permute-start | bytes 786440 | tf_op jit(solution)/shard_map/ppermute | solution.py:153
  121.9 11.5 %collective-permute-start = (bf16[128,4096]{1,0:T(8,128)(2,1)S(1)}, bf16[128,4096]{1,0:T(8,128)(2,1)S(1)}, u32[]{:S(2)}, u32[]{:S(2)}) collective-permute-start(bf16[128,4096]{1,0:T(8,128)(2,1)S(1)} %copy-done), channel_id=1, source_target_pairs={{0,1},{1,0},{2,3},{3,2},{4,5},{5,4},{6,7},{7,6},{8,9},{9,8},{10,11... | collective-permute-start | bytes 3145736 | tf_op jit(solution)/shard_map/ppermute | solution.py:153
  122.7 10.7 %collective-permute-start.7 = (bf16[128,4096]{1,0:T(8,128)(2,1)S(1)}, bf16[128,4096]{1,0:T(8,128)(2,1)S(1)}, u32[]{:S(2)}, u32[]{:S(2)}) collective-permute-start(bf16[128,4096]{1,0:T(8,128)(2,1)S(1)} %copy-done.1), channel_id=1, source_target_pairs={{0,1},{1,0},{2,3},{3,2},{4,5},{5,4},{6,7},{7,6},{8,9},{9,8},{10,11... | collective-permute-start | bytes 3145736 | tf_op jit(solution)/shard_map/ppermute | solution.py:153
  128.2 18.1 %copy-start.13 = (bf16[32,4096]{1,0:T(8,128)(2,1)}, bf16[32,4096]{1,0:T(8,128)(2,1)S(1)}, u32[]{:S(2)}) copy-start(bf16[32,4096]{1,0:T(8,128)(2,1)S(1)} %collective-permute-done.21.refs_6_) | copy-start | bytes 786436
  128.2 2.5 %collective-permute-start.16 = (bf16[128,2048]{1,0:T(8,128)(2,1)S(1)}, bf16[128,2048]{1,0:T(8,128)(2,1)S(1)}, u32[]{:S(2)}, u32[]{:S(2)}) collective-permute-start(bf16[128,2048]{1,0:T(8,128)(2,1)S(1)} %broadcast_select_fusion), channel_id=1, source_target_pairs={{0,1},{1,0},{2,3},{3,2},{4,5},{5,4},{6,7},{7,6},{8,9},{9,8},{10,11... | collective-permute-start | bytes 1572872 | tf_op jit(solution)/shard_map/ppermute | solution.py:153
  129.2 5.6 %collective-permute-start.10 = (bf16[128,2048]{1,0:T(8,128)(2,1)S(1)}, bf16[128,2048]{1,0:T(8,128)(2,1)S(1)}, u32[]{:S(2)}, u32[]{:S(2)}) collective-permute-start(bf16[128,2048]{1,0:T(8,128)(2,1)S(1)} %broadcast_select_fusion.2), channel_id=1, source_target_pairs={{0,1},{1,0},{2,3},{3,2},{4,5},{5,4},{6,7},{7,6},{8,9},{9,8},{10,11... | collective-permute-start | bytes 1572872 | tf_op jit(solution)/shard_map/ppermute | solution.py:153
  129.4 5.7 %collective-permute-start.6 = (bf16[128,2048]{1,0:T(8,128)(2,1)S(1)}, bf16[128,2048]{1,0:T(8,128)(2,1)S(1)}, u32[]{:S(2)}, u32[]{:S(2)}) collective-permute-start(bf16[128,2048]{1,0:T(8,128)(2,1)S(1)} %broadcast_select_fusion.3), channel_id=1, source_target_pairs={{0,1},{1,0},{2,3},{3,2},{4,5},{5,4},{6,7},{7,6},{8,9},{9,8},{10,11... | collective-permute-start | bytes 1572872 | tf_op jit(solution)/shard_map/ppermute | solution.py:153
  130.8 5.9 %collective-permute-start.25 = (bf16[32,4096]{1,0:T(8,128)(2,1)S(1)}, bf16[32,4096]{1,0:T(8,128)(2,1)}, u32[]{:S(2)}, u32[]{:S(2)}) collective-permute-start(bf16[32,4096]{1,0:T(8,128)(2,1)S(1)} %broadcast_select_fusion.4), channel_id=1, source_target_pairs={{0,2},{2,4},{4,6},{6,8},{8,10},{10,12},{12,14},{14,16},{16,18},{18... | collective-permute-start | bytes 786440 | tf_op jit(solution)/shard_map/ppermute | solution.py:153
  133.3 19.0 %collective-permute-start.28 = (bf16[32,4096]{1,0:T(8,128)(2,1)}, bf16[32,4096]{1,0:T(8,128)(2,1)S(1)}, u32[]{:S(2)}, u32[]{:S(2)}) collective-permute-start(bf16[32,4096]{1,0:T(8,128)(2,1)} %collective-permute-done.20.refs_5_), channel_id=1, source_target_pairs={{0,1},{1,0},{2,3},{3,2},{4,5},{5,4},{6,7},{7,6},{8,9},{9,8},{10,11... | collective-permute-start | bytes 786440 | tf_op jit(solution)/shard_map/ppermute | solution.py:153
  134.4 18.0 %collective-permute-start.31 = (bf16[32,4096]{1,0:T(8,128)(2,1)}, bf16[32,4096]{1,0:T(8,128)(2,1)S(1)}, u32[]{:S(2)}, u32[]{:S(2)}) collective-permute-start(bf16[32,4096]{1,0:T(8,128)(2,1)} %collective-permute-done.23.refs_8_), channel_id=1, source_target_pairs={{0,1},{1,0},{2,3},{3,2},{4,5},{5,4},{6,7},{7,6},{8,9},{9,8},{10,11... | collective-permute-start | bytes 786440 | tf_op jit(solution)/shard_map/ppermute | solution.py:153
  134.8 17.5 %collective-permute-start.29 = (bf16[32,4096]{1,0:T(8,128)(2,1)S(1)}, bf16[32,4096]{1,0:T(8,128)(2,1)S(1)}, u32[]{:S(2)}, u32[]{:S(2)}) collective-permute-start(bf16[32,4096]{1,0:T(8,128)(2,1)S(1)} %collective-permute-done.21.refs_6_), channel_id=1, source_target_pairs={{0,1},{1,0},{2,3},{3,2},{4,5},{5,4},{6,7},{7,6},{8,9},{9,8},{10,11... | collective-permute-start | bytes 786440 | tf_op jit(solution)/shard_map/ppermute | solution.py:153
  135.0 17.4 %collective-permute-start.32 = (bf16[32,4096]{1,0:T(8,128)(2,1)}, bf16[32,4096]{1,0:T(8,128)(2,1)S(1)}, u32[]{:S(2)}, u32[]{:S(2)}) collective-permute-start(bf16[32,4096]{1,0:T(8,128)(2,1)} %collective-permute-done.24.refs_9_), channel_id=1, source_target_pairs={{0,1},{1,0},{2,3},{3,2},{4,5},{5,4},{6,7},{7,6},{8,9},{9,8},{10,11... | collective-permute-start | bytes 786440 | tf_op jit(solution)/shard_map/ppermute | solution.py:153
  136.7 15.8 %collective-permute-start.33 = (bf16[32,4096]{1,0:T(8,128)(2,1)}, bf16[32,4096]{1,0:T(8,128)(2,1)S(1)}, u32[]{:S(2)}, u32[]{:S(2)}) collective-permute-start(bf16[32,4096]{1,0:T(8,128)(2,1)} %collective-permute-done.25.refs_10_), channel_id=1, source_target_pairs={{0,1},{1,0},{2,3},{3,2},{4,5},{5,4},{6,7},{7,6},{8,9},{9,8},{10,11... | collective-permute-start | bytes 786440 | tf_op jit(solution)/shard_map/ppermute | solution.py:153
  (13 other events, 44.5 us)
